TPU v7x, 32 devices: a 4x2x2 block of a 4x4x8 slice. The times are simulated.
32 devices in a mesh: dp: 4 (over y, z), tp: 8 (over x, core).
Axes of the slice: x: 4, y: 2, z: 2, core: 2. Of those that a mesh axis runs over, the one named last changes fastest.
The devices are a block of a 4x4x8 slice.
Arguments:
- tokens: int32 [4, 128], P('dp'), parts along dimension 0
- positions: int32 [4, 128], P('dp'), parts along dimension 0
- embedding: bfloat16 [16384, 2048], P('tp')
- gain_attn: float32 [2048], replicated
- gain_mlp: float32 [2048], replicated
- w_query: bfloat16 [2048, 16, 128], P(None, 'tp')
- w_key: bfloat16 [2048, 8, 128], P(None, 'tp')
- w_value: bfloat16 [2048, 8, 128], P(None, 'tp')
- w_out: bfloat16 [16, 128, 2048], P('tp')
- w_gate: bfloat16 [2048, 6144], P(None, 'tp')
- w_up: bfloat16 [2048, 6144], P(None, 'tp')
- w_down: bfloat16 [6144, 2048], P('tp')
- grad_hidden: bfloat16 [4, 128, 2048], P('dp', 'tp'), parts along dimension 0
Outputs:
- output 1: bfloat16 [4, 128, 2048], P('dp', 'tp'), parts along dimension 0
- output 2: float32 [65536, 2048], P(('dp', 'tp')), parts along dimension 0
- output 3: float32 [8192, 16, 128], P('dp', 'tp'), parts along dimension 0
- output 4: float32 [8192, 8, 128], P('dp', 'tp'), parts along dimension 0
- output 5: float32 [8192, 8, 128], P('dp', 'tp'), parts along dimension 0
- output 6: float32 [64, 128, 2048], P(('dp', 'tp')), parts along dimension 0
- output 7: float32 [8192, 6144], P('dp', 'tp'), parts along dimension 0
- output 8: float32 [8192, 6144], P('dp', 'tp'), parts along dimension 0
- output 9: float32 [24576, 2048], P(('dp', 'tp')), parts along dimension 0
- output 10: float32 [8192], P('dp'), parts along dimension 0
- output 11: float32 [8192], P('dp'), parts along dimension 0
There are 4 independent parts. A program takes and returns all parts, laid end to end along the dimension named above; an argument that names none is the same for every part.
All inputs are finite; a program needn't handle non-finite values.
Results may differ from a plain program's by a relative error of at most 0.02.
Values are sent between devices in bfloat16 or wider.
A program may use at most 768 MiB of HBM per device.

v0:
```python
import jax
import jax.numpy as jnp
from jax import lax
from jax.sharding import PartitionSpec as P

ROPE_THETA = 1000000.0
RMS_EPS = 1e-5


def rope_tables(positions, head_dim):
    half_dim = head_dim // 2
    inv_freq = ROPE_THETA ** (-jnp.arange(half_dim, dtype=jnp.float32) * (2.0 / head_dim))
    angles = positions.astype(jnp.float32)[:, :, None] * inv_freq
    return jnp.cos(angles)[:, :, None, :], jnp.sin(angles)[:, :, None, :]


def rotate(values, cos_tab, sin_tab):
    half_dim = values.shape[-1] // 2
    first_half = values[..., :half_dim]
    second_half = values[..., half_dim:]
    return jnp.concatenate([first_half * cos_tab - second_half * sin_tab, second_half * cos_tab + first_half * sin_tab], axis=-1)


def norm_fwd(hidden, gain_vec):
    hidden_f = hidden.astype(jnp.float32)
    inv_rms = lax.rsqrt(jnp.mean(hidden_f * hidden_f, axis=-1, keepdims=True) + RMS_EPS)
    normed = hidden_f * inv_rms
    return (normed * gain_vec).astype(jnp.bfloat16), normed, inv_rms


def norm_bwd(grad_normed, normed, inv_rms, gain_vec):
    grad_f = grad_normed.astype(jnp.float32)
    gain_part = jnp.sum(grad_f * normed, axis=(0, 1))
    scaled = grad_f * gain_vec
    grad_in = inv_rms * (scaled - normed * jnp.mean(scaled * normed, axis=-1, keepdims=True))
    return grad_in, gain_part


def layer_pass(first_x, positions, gain_attn, gain_mlp, w_query, w_key, w_value, w_out, w_gate, w_up, w_down, grad_hidden):
    batch_size, seq_len = positions.shape
    local_heads, head_dim = w_query.shape[1], w_query.shape[2]
    local_kv = w_key.shape[1]
    group_size = local_heads // local_kv
    score_scale = head_dim ** -0.5
    cos_tab, sin_tab = rope_tables(positions, head_dim)
    normed1_bf, normed1, inv_rms1 = norm_fwd(first_x, gain_attn)
    gathered1 = lax.all_gather(normed1_bf, 'tp', axis=1, tiled=True)
    queries = rotate(jnp.einsum('bsd,dhe->bshe', gathered1, w_query, preferred_element_type=jnp.float32), cos_tab, sin_tab).astype(jnp.bfloat16)
    keys_rot = rotate(jnp.einsum('bsd,dhe->bshe', gathered1, w_key, preferred_element_type=jnp.float32), cos_tab, sin_tab).astype(jnp.bfloat16)
    values = jnp.einsum('bsd,dhe->bshe', gathered1, w_value, preferred_element_type=jnp.float32).astype(jnp.bfloat16)
    queries5 = queries.reshape(batch_size, seq_len, local_kv, group_size, head_dim)
    causal = jnp.arange(seq_len)[:, None] >= jnp.arange(seq_len)[None, :]
    scores = jnp.einsum('bqkgd,bskd->bkgqs', queries5, keys_rot, preferred_element_type=jnp.float32) * score_scale
    probs_f = jax.nn.softmax(jnp.where(causal, scores, -1e30), axis=-1)
    probs_bf = probs_f.astype(jnp.bfloat16)
    attn_heads = jnp.einsum('bkgqs,bskd->bqkgd', probs_bf, values, preferred_element_type=jnp.float32)
    attn_heads = attn_heads.astype(jnp.bfloat16).reshape(batch_size, seq_len, local_heads, head_dim)
    attn_part = jnp.einsum('bshe,hed->bsd', attn_heads, w_out, preferred_element_type=jnp.float32).astype(jnp.bfloat16)
    attn_sum = lax.psum_scatter(attn_part, 'tp', scatter_dimension=1, tiled=True)
    hidden1 = (first_x.astype(jnp.float32) + attn_sum.astype(jnp.float32)).astype(jnp.bfloat16)
    normed2_bf, normed2, inv_rms2 = norm_fwd(hidden1, gain_mlp)
    gathered2 = lax.all_gather(normed2_bf, 'tp', axis=1, tiled=True)
    gate_pre = jnp.einsum('bsd,df->bsf', gathered2, w_gate, preferred_element_type=jnp.float32)
    up_pre = jnp.einsum('bsd,df->bsf', gathered2, w_up, preferred_element_type=jnp.float32)
    gate_sig = jax.nn.sigmoid(gate_pre)
    gate_act = gate_pre * gate_sig
    act_bf = (gate_act * up_pre).astype(jnp.bfloat16)
    mlp_part = jnp.einsum('bsf,fd->bsd', act_bf, w_down, preferred_element_type=jnp.float32).astype(jnp.bfloat16)
    mlp_sum = lax.psum_scatter(mlp_part, 'tp', scatter_dimension=1, tiled=True)
    hidden_out = (hidden1.astype(jnp.float32) + mlp_sum.astype(jnp.float32)).astype(jnp.bfloat16)

    grad_full = lax.all_gather(grad_hidden, 'tp', axis=1, tiled=True)
    grad_act = jnp.einsum('bsd,fd->bsf', grad_full, w_down, preferred_element_type=jnp.float32).astype(jnp.bfloat16).astype(jnp.float32)
    grad_up = (grad_act * gate_act).astype(jnp.bfloat16)
    grad_gate = (grad_act * up_pre * gate_sig * (1.0 + gate_pre * (1.0 - gate_sig))).astype(jnp.bfloat16)
    grad_w_down = jnp.einsum('bsf,bsd->fd', act_bf, grad_full, preferred_element_type=jnp.float32)
    grad_w_gate = jnp.einsum('bsd,bsf->df', gathered2, grad_gate, preferred_element_type=jnp.float32)
    grad_w_up = jnp.einsum('bsd,bsf->df', gathered2, grad_up, preferred_element_type=jnp.float32)
    grad_n2_part = (jnp.einsum('bsf,df->bsd', grad_gate, w_gate, preferred_element_type=jnp.float32) + jnp.einsum('bsf,df->bsd', grad_up, w_up, preferred_element_type=jnp.float32)).astype(jnp.bfloat16)
    grad_n2 = lax.psum_scatter(grad_n2_part, 'tp', scatter_dimension=1, tiled=True)
    grad_h1_norm, gain_mlp_part = norm_bwd(grad_n2, normed2, inv_rms2, gain_mlp)
    grad_h1 = (grad_hidden.astype(jnp.float32) + grad_h1_norm).astype(jnp.bfloat16)
    grad_h1_full = lax.all_gather(grad_h1, 'tp', axis=1, tiled=True)
    grad_heads = jnp.einsum('bsd,hed->bshe', grad_h1_full, w_out, preferred_element_type=jnp.float32).astype(jnp.bfloat16)
    grad_w_out = jnp.einsum('bshe,bsd->hed', attn_heads, grad_h1_full, preferred_element_type=jnp.float32)
    grad_heads5 = grad_heads.reshape(batch_size, seq_len, local_kv, group_size, head_dim)
    grad_probs = jnp.einsum('bqkgd,bskd->bkgqs', grad_heads5, values, preferred_element_type=jnp.float32).astype(jnp.bfloat16).astype(jnp.float32)
    grad_values = jnp.einsum('bkgqs,bqkgd->bskd', probs_bf, grad_heads5, preferred_element_type=jnp.float32).astype(jnp.bfloat16)
    grad_scores = (probs_f * (grad_probs - jnp.sum(grad_probs * probs_f, axis=-1, keepdims=True)) * score_scale).astype(jnp.bfloat16)
    grad_queries = jnp.einsum('bkgqs,bskd->bqkgd', grad_scores, keys_rot, preferred_element_type=jnp.float32).astype(jnp.bfloat16)
    grad_queries = grad_queries.reshape(batch_size, seq_len, local_heads, head_dim)
    grad_keys = jnp.einsum('bkgqs,bqkgd->bskd', grad_scores, queries5, preferred_element_type=jnp.float32).astype(jnp.bfloat16)
    grad_q_lin = rotate(grad_queries.astype(jnp.float32), cos_tab, -sin_tab).astype(jnp.bfloat16)
    grad_k_lin = rotate(grad_keys.astype(jnp.float32), cos_tab, -sin_tab).astype(jnp.bfloat16)
    grad_w_query = jnp.einsum('bsd,bshe->dhe', gathered1, grad_q_lin, preferred_element_type=jnp.float32)
    grad_w_key = jnp.einsum('bsd,bshe->dhe', gathered1, grad_k_lin, preferred_element_type=jnp.float32)
    grad_w_value = jnp.einsum('bsd,bshe->dhe', gathered1, grad_values, preferred_element_type=jnp.float32)
    grad_n1_part = (jnp.einsum('bshe,dhe->bsd', grad_q_lin, w_query, preferred_element_type=jnp.float32)
                    + jnp.einsum('bshe,dhe->bsd', grad_k_lin, w_key, preferred_element_type=jnp.float32)
                    + jnp.einsum('bshe,dhe->bsd', grad_values, w_value, preferred_element_type=jnp.float32)).astype(jnp.bfloat16)
    grad_n1 = lax.psum_scatter(grad_n1_part, 'tp', scatter_dimension=1, tiled=True)
    grad_x_norm, gain_attn_part = norm_bwd(grad_n1, normed1, inv_rms1, gain_attn)
    grad_first = (grad_h1.astype(jnp.float32) + grad_x_norm).astype(jnp.bfloat16)
    gain_grads = lax.psum(jnp.stack([gain_attn_part, gain_mlp_part]), 'tp')
    grad_weights = (grad_w_query, grad_w_key, grad_w_value, grad_w_out, grad_w_gate, grad_w_up, grad_w_down)
    return hidden_out, grad_first, grad_weights, gain_grads


def solution(mesh):
    in_specs = (P('dp', None), P('dp', None), P('tp', None), P(None), P(None),
                P(None, 'tp', None), P(None, 'tp', None), P(None, 'tp', None), P('tp', None, None),
                P(None, 'tp'), P(None, 'tp'), P('tp', None), P('dp', 'tp', None))
    out_specs = (P('dp', 'tp', None), P(('dp', 'tp'), None),
                 P('dp', 'tp', None), P('dp', 'tp', None), P('dp', 'tp', None), P(('dp', 'tp'), None, None),
                 P('dp', 'tp'), P('dp', 'tp'), P(('dp', 'tp'), None), P('dp'), P('dp'))

    def device_fn(tokens, positions, emb_shard, gain_attn, gain_mlp, w_query, w_key, w_value, w_out, w_gate, w_up, w_down, grad_hidden):
        rows_local = emb_shard.shape[0]
        local_ids = tokens - lax.axis_index('tp') * rows_local
        owned_row = (local_ids >= 0) & (local_ids < rows_local)
        looked_up = jnp.take(emb_shard, jnp.clip(local_ids, 0, rows_local - 1), axis=0)
        partial_emb = jnp.where(owned_row[:, :, None], looked_up, jnp.zeros((), jnp.bfloat16))
        first_x = lax.psum_scatter(partial_emb, 'tp', scatter_dimension=1, tiled=True)
        hidden_out, grad_first, grad_weights, gain_grads = layer_pass(
            first_x, positions, gain_attn, gain_mlp, w_query, w_key, w_value, w_out, w_gate, w_up, w_down, grad_hidden)
        grad_first_full = lax.all_gather(grad_first, 'tp', axis=1, tiled=True)
        seg_ids = jnp.where(owned_row, local_ids, rows_local).reshape(-1)
        grad_embedding = jax.ops.segment_sum(grad_first_full.reshape(-1, grad_first_full.shape[-1]).astype(jnp.float32), seg_ids, num_segments=rows_local)
        return (hidden_out, grad_embedding) + grad_weights + (gain_grads[0], gain_grads[1])

    return jax.shard_map(device_fn, mesh=mesh, in_specs=in_specs, out_specs=out_specs, check_vma=False)
```

profile of v0, /device:TPU:81, one launch (start us, length us, event | category | flops | bytes accessed | tf_op | source)
XLA Modules:
  0.0 288.0 jit_solution(4718844712808129949)
XLA Ops:
  7.3 1.4 select_bitcast_fusion
  8.7 6.7 %gather_fusion = bf16[128,2048]{1,0:T(8,128)(2,1)} fusion(bf16[2048,2048]{1,0:T(8,128)(2,1)} %param.15, s32[1024]{0:T(1024)S(1)} %pad_clamp_fusion), kind=kCustom, calls=%fused_computation | custom fusion | bytes 1049088 | tf_op jit(solution)/shard_map/jit(_take)/gather | solution.py:121
  15.4 2.0 fusion.56
  17.5 3.7 %copy.41 = bf16[2048,2,128]{0,2,1:T(8,128)(2,1)} copy(bf16[2048,2,128]{2,1,0:T(2,128)(2,1)} %param.18) | data formatting | bytes 2097152 | tf_op args[5]
  21.5 25.7 %reduce-scatter.6.cloned.1.call-done = bf16[1,16,2048]{2,1,0:T(8,128)(2,1)} async-done(((bf16[1,128,2048]{2,1,0:T(8,128)(2,1)}), bf16[1,16,2048]{2,1,0:T(8,128)(2,1)}) %reduce-scatter.6.cloned.1.call-update) | async-done | bytes 65552 | tf_op jit(solution)/shard_map/reduce_scatter | solution.py:123
  47.2 1.1 fusion.77
  48.3 0.9 fusion.74
  49.2 16.5 %all_gather.15 = bf16[1,128,2048]{2,1,0:T(8,128)(2,1)S(1)} all-gather(bf16[1,16,2048]{2,1,0:T(8,128)(2,1)S(1)} %fusion.74), channel_id=1, replica_groups=mesh['dp'=4,'tp'=8] {'tp'}, dimensions={1}, use_global_device_ids=true | all-gather | bytes 589824 | tf_op jit(solution)/shard_map/all_gather | solution.py:47
  65.7 1.5 fusion.21
  67.3 1.4 convolution_bitcast_fusion.4
  70.6 1.1 fusion.8
  71.8 13.1 %all_gather.17 = bf16[1,128,2048]{2,1,0:T(8,128)(2,1)} all-gather(bf16[1,16,2048]{2,1,0:T(8,128)(2,1)S(1)} %copy-done.22), channel_id=1, replica_groups=mesh['dp'=4,'tp'=8] {'tp'}, dimensions={1}, use_global_device_ids=true | all-gather | bytes 589824 | tf_op jit(solution)/shard_map/all_gather | solution.py:72
  85.0 11.6 %reduce-scatter.8.cloned.1.call-done = bf16[1,16,2048]{2,1,0:T(8,128)(2,1)} async-done(((bf16[1,128,2048]{2,1,0:T(8,128)(2,1)}), bf16[1,16,2048]{2,1,0:T(8,128)(2,1)}) %reduce-scatter.8.cloned.1.call-update) | async-done | bytes 65552 | tf_op jit(solution)/shard_map/reduce_scatter | solution.py:59
  96.6 1.1 fusion.82
  97.8 16.5 %all_gather.16 = bf16[1,128,2048]{2,1,0:T(8,128)(2,1)S(1)} all-gather(bf16[1,16,2048]{2,1,0:T(8,128)(2,1)S(1)} %fusion.79), channel_id=1, replica_groups=mesh['dp'=4,'tp'=8] {'tp'}, dimensions={1}, use_global_device_ids=true | all-gather | bytes 589824 | tf_op jit(solution)/shard_map/all_gather | solution.py:62
  114.4 2.7 fusion.40
  117.1 0.6 fusion.42
  117.8 1.2 multiply_convert_fusion
  119.0 1.1 fusion.131
  120.2 0.9 copy-done.6
  121.1 1.9 fusion.7
  123.1 1.4 fusion.5
  124.5 4.8 %fusion.33 = f32[768,2048]{1,0:T(8,128)} fusion(bf16[128,768]{1,0:T(8,128)(2,1)S(1)} %get-tuple-element.43, bf16[1,128,2048]{2,1,0:T(8,128)(2,1)} %all_gather.17), kind=kOutput, calls=%fused_computation.51 | convolution fusion | flops 402653184 | bytes 7012352 | tf_op jit(solution)/shard_map/bsf,bsd->fd/dot_general | solution.py:76
  129.5 3.7 %fusion.36 = f32[2048,768]{1,0:T(8,128)} fusion(bf16[128,768]{1,0:T(8,128)(2,1)S(1)} %copy-done.19, bf16[1,128,2048]{2,1,0:T(8,128)(2,1)S(1)} %copy-done.5), kind=kOutput, calls=%fused_computation.54 | convolution fusion | flops 402653184 | bytes 7012352 | tf_op jit(solution)/shard_map/bsd,bsf->df/dot_general | solution.py:78
  133.2 3.7 %fusion.38 = f32[2048,768]{1,0:T(8,128)} fusion(bf16[128,768]{1,0:T(8,128)(2,1)S(1)} %copy-done.17, bf16[1,128,2048]{2,1,0:T(8,128)(2,1)S(1)} %copy-done.5), kind=kOutput, calls=%fused_computation.56 | convolution fusion | flops 402653184 | bytes 7012352 | tf_op jit(solution)/shard_map/bsd,bsf->df/dot_general | solution.py:77
  136.9 11.0 %reduce-scatter.12.cloned.1.call-done = bf16[1,16,2048]{2,1,0:T(8,128)(2,1)} async-done(((bf16[1,128,2048]{2,1,0:T(8,128)(2,1)}), bf16[1,16,2048]{2,1,0:T(8,128)(2,1)}) %reduce-scatter.12.cloned.1.call-update) | async-done | bytes 65552 | tf_op jit(solution)/shard_map/reduce_scatter | solution.py:80
  147.9 1.5 fusion.81
  149.5 28.2 %reduce-scatter.10.cloned.1.call-done = bf16[1,16,2048]{2,1,0:T(8,128)(2,1)} async-done(((bf16[1,128,2048]{2,1,0:T(8,128)(2,1)}), bf16[1,16,2048]{2,1,0:T(8,128)(2,1)}) %reduce-scatter.10.cloned.1.call-update) | async-done | bytes 65552 | tf_op jit(solution)/shard_map/reduce_scatter | solution.py:69
  177.6 1.5 fusion.73
  179.1 16.6 %all_gather.18 = bf16[1,128,2048]{2,1,0:T(8,128)(2,1)S(1)} all-gather(bf16[1,16,2048]{2,1,0:T(8,128)(2,1)S(1)} %get-tuple-element.52), channel_id=1, replica_groups=mesh['dp'=4,'tp'=8] {'tp'}, dimensions={1}, use_global_device_ids=true | all-gather | bytes 589824 | tf_op jit(solution)/shard_map/all_gather | solution.py:83
  196.3 1.1 fusion.22
  197.4 1.0 multiply_reduce_fusion
  198.4 0.7 fusion.86
  199.2 0.9 fusion.25
  200.1 0.9 fusion.18
  201.0 0.9 fusion.115
  202.6 1.1 fusion.6
  204.3 8.6 %copy.55 = f32[2048,2,128]{2,1,0:T(2,128)} copy(f32[2048,2,128]{2,0,1:T(8,128)S(1)} %fusion.27) | data formatting | bytes 4194304
  212.9 1.3 fusion.48
  214.2 1.3 fusion.50
  215.5 1.7 fusion.30
  217.2 11.4 %reduce-scatter.14.cloned.1.call-done = bf16[1,16,2048]{2,1,0:T(8,128)(2,1)} async-done(((bf16[1,128,2048]{2,1,0:T(8,128)(2,1)}), bf16[1,16,2048]{2,1,0:T(8,128)(2,1)}) %reduce-scatter.14.cloned.1.call-update) | async-done | bytes 65552 | tf_op jit(solution)/shard_map/reduce_scatter | solution.py:101
  228.6 1.1 fusion.76
  229.7 23.5 %psum.7 = f32[2,2048]{1,0:T(2,128)S(1)} all-reduce(f32[2,2048]{1,0:T(2,128)S(1)} %pad_maximum_fusion.9), channel_id=1, replica_groups=mesh['dp'=4,'tp'=8] {'tp'}, use_global_device_ids=true, to_apply=%region_15.16 | all-reduce | flops 4096 | bytes 32768 | tf_op jit(solution)/shard_map/psum | solution.py:104
  253.2 0.6 fusion.129
  253.8 0.9 fusion.70
  254.7 16.8 %all_gather.19 = bf16[1,128,2048]{2,1,0:T(8,128)(2,1)} all-gather(bf16[1,16,2048]{2,1,0:T(8,128)(2,1)S(1)} %fusion.70), channel_id=1, replica_groups=mesh['dp'=4,'tp'=8] {'tp'}, dimensions={1}, use_global_device_ids=true | all-gather | bytes 589824 | tf_op jit(solution)/shard_map/all_gather | solution.py:126
  271.5 9.9 %scatter_custom_fusion = f32[2048,2048]{1,0:T(8,128)} fusion(s32[128]{0:T(128)} %get-tuple-element.37, f32[]{:T(128)} %constant.21.clone.1, bf16[1,128,2048]{2,1,0:T(8,128)(2,1)} %all_gather.19), kind=kCustom, calls=%fused_computation.2 | custom fusion | flops 524288 | bytes 17302016 | tf_op jit(solution)/shard_map/scatter-add | solution.py:128
  (119 shorter events, 4.5 us)
Async XLA Ops:
  7.2 110.5 %copy-start = (bf16[768,2048]{1,0:T(8,128)(2,1)S(1)}, bf16[768,2048]{1,0:T(8,128)(2,1)}, u32[]{:S(2)}) copy-start(bf16[768,2048]{1,0:T(8,128)(2,1)} %param.24) | copy-start | bytes 9437188
  7.2 39.9 %reduce-scatter.6.cloned.1.call-start = ((), (), s32[]{:S(2)}) async-start(), calls=%async_computation.5 | async-start | bytes 589824 | tf_op jit(solution)/shard_map/reduce_scatter | solution.py:123
  8.7 12.5 %copy-start.42 = (s32[1,128]{1,0:T(1,128)S(1)}, s32[1,128]{1,0:T(1,128)}, u32[]{:S(2)}) copy-start(s32[1,128]{1,0:T(1,128)} %param.14) | copy-start | bytes 1540
  8.7 39.6 %copy-start.29 = (f32[2048]{0:T(1024)S(1)}, f32[2048]{0:T(1024)}, u32[]{:S(2)}) copy-start(f32[2048]{0:T(1024)} %param.16) | copy-start | bytes 24580
  17.5 79.1 %reduce-scatter.8.cloned.1.call-start = ((), (), s32[]{:S(2)}) async-start(), calls=%async_computation.6 | async-start | bytes 589824 | tf_op jit(solution)/shard_map/reduce_scatter | solution.py:59
  21.2 50.5 %copy-start.36 = (f32[64]{0:T(128)}, f32[64]{0:T(128)S(1)}, u32[]{:S(2)}) copy-start(f32[64]{0:T(128)S(1)} %multiply_power_fusion) | copy-start | bytes 772
  21.3 50.4 %copy-start.37 = (f32[128]{0:T(128)}, f32[128]{0:T(128)S(1)}, u32[]{:S(2)}) copy-start(f32[128]{0:T(128)S(1)} %convert_bitcast_fusion) | copy-start | bytes 1540
  47.1 21.8 %copy-start.8 = (bf16[2048,2,128]{0,2,1:T(8,128)(2,1)S(1)}, bf16[2048,2,128]{0,2,1:T(8,128)(2,1)}, u32[]{:S(2)}) copy-start(bf16[2048,2,128]{0,2,1:T(8,128)(2,1)} %copy.41) | copy-start | bytes 3145732
  47.1 23.4 %copy-start.10 = (bf16[2,128,2048]{2,1,0:T(8,128)(2,1)S(1)}, bf16[2,128,2048]{2,1,0:T(8,128)(2,1)}, u32[]{:S(2)}) copy-start(bf16[2,128,2048]{2,1,0:T(8,128)(2,1)} %param.21) | copy-start | bytes 3145732
  48.3 19.0 %copy-start.34 = (f32[16]{0:T(128)}, f32[16]{0:T(128)S(1)}, u32[]{:S(2)}) copy-start(f32[16]{0:T(128)S(1)} %add_rsqrt_fusion.1) | copy-start | bytes 196
  65.7 3.2 %copy-start.2 = (bf16[1,128,2048]{2,1,0:T(8,128)(2,1)}, bf16[1,128,2048]{2,1,0:T(8,128)(2,1)S(1)}, u32[]{:S(2)}) copy-start(bf16[1,128,2048]{2,1,0:T(8,128)(2,1)S(1)} %all_gather.15) | copy-start | bytes 1572868
  67.3 17.7 %copy-start.32 = (bf16[128,128,1]{1,0,2:T(8,128)(2,1)}, bf16[128,128,1]{1,0,2:T(8,128)(2,1)S(1)}, u32[]{:S(2)}) copy-start(bf16[128,128,1]{1,0,2:T(8,128)(2,1)S(1)} %fusion.21) | copy-start | bytes 98308
  67.3 4.6 %copy-start.22 = (bf16[1,16,2048]{2,1,0:T(8,128)(2,1)S(1)}, bf16[1,16,2048]{2,1,0:T(8,128)(2,1)}, u32[]{:S(2)}) copy-start(bf16[1,16,2048]{2,1,0:T(8,128)(2,1)} %param.25) | copy-start | bytes 196612
  68.7 27.9 %copy-start.15 = (bf16[1,16,2048]{2,1,0:T(8,128)(2,1)S(1)}, bf16[1,16,2048]{2,1,0:T(8,128)(2,1)}, u32[]{:S(2)}) copy-start(bf16[1,16,2048]{2,1,0:T(8,128)(2,1)} %reduce-scatter.6.cloned.1.call-done) | copy-start | bytes 196612
  68.7 29.0 %copy-start.28 = (f32[2048]{0:T(1024)S(1)}, f32[2048]{0:T(1024)}, u32[]{:S(2)}) copy-start(f32[2048]{0:T(1024)} %param.17) | copy-start | bytes 24580
  68.9 45.4 %copy-start.30 = (bf16[128,64]{0,1:T(8,128)(2,1)}, bf16[128,64]{0,1:T(8,128)(2,1)S(1)}, u32[]{:S(2)}) copy-start(bf16[128,64]{0,1:T(8,128)(2,1)S(1)} %get-tuple-element.50) | copy-start | bytes 49156
  69.0 45.4 %copy-start.31 = (bf16[128,64]{0,1:T(8,128)(2,1)}, bf16[128,64]{0,1:T(8,128)(2,1)S(1)}, u32[]{:S(2)}) copy-start(bf16[128,64]{0,1:T(8,128)(2,1)S(1)} %get-tuple-element.51) | copy-start | bytes 49156
  69.5 0.6 copy-start.26
  69.5 0.6 copy-start.27
  69.7 0.7 copy-start.20
  69.7 15.3 %copy-start.40 = (f32[2,128]{1,0:T(2,128)}, f32[2,128]{1,0:T(2,128)S(1)}, u32[]{:S(2)}) copy-start(f32[2,128]{1,0:T(2,128)S(1)} %get-tuple-element.61) | copy-start | bytes 3076
  70.3 14.6 %copy-start.41 = (f32[2,128]{1,0:T(2,128)}, f32[2,128]{1,0:T(2,128)S(1)}, u32[]{:S(2)}) copy-start(f32[2,128]{1,0:T(2,128)S(1)} %fusion.85) | copy-start | bytes 3076
  70.6 46.5 %copy-start.24 = (bf16[128,2,128]{0,2,1:T(8,128)(2,1)}, bf16[128,2,128]{0,2,1:T(8,128)(2,1)S(1)}, u32[]{:S(2)}) copy-start(bf16[128,2,128]{0,2,1:T(8,128)(2,1)S(1)} %fusion.12) | copy-start | bytes 196612
  71.8 76.1 %reduce-scatter.12.cloned.1.call-start = ((), (), s32[]{:S(2)}) async-start(), calls=%async_computation.8 | async-start | bytes 589824 | tf_op jit(solution)/shard_map/reduce_scatter | solution.py:80
  96.6 20.5 %copy-start.7 = (bf16[2048,768]{1,0:T(8,128)(2,1)S(1)}, bf16[2048,768]{1,0:T(8,128)(2,1)}, u32[]{:S(2)}) copy-start(bf16[2048,768]{1,0:T(8,128)(2,1)} %param.22) | copy-start | bytes 9437188
  97.7 19.3 %copy-start.38 = (f32[16]{0:T(128)}, f32[16]{0:T(128)S(1)}, u32[]{:S(2)}) copy-start(f32[16]{0:T(128)S(1)} %add_rsqrt_fusion) | copy-start | bytes 196
  114.4 2.7 copy-start.4
  114.4 3.4 %copy-start.12 = (bf16[1,128,2048]{2,1,0:T(8,128)(2,1)S(1)}, bf16[1,128,2048]{2,1,0:T(8,128)(2,1)}, u32[]{:S(2)}) copy-start(bf16[1,128,2048]{2,1,0:T(8,128)(2,1)} %all_gather.17) | copy-start | bytes 1572868
  119.0 1.2 copy-start.16
  119.0 1.2 copy-start.18
  119.0 2.0 copy-start.6
  123.1 54.6 %reduce-scatter.10.cloned.1.call-start = ((), (), s32[]{:S(2)}) async-start(), calls=%async_computation.7 | async-start | bytes 589824 | tf_op jit(solution)/shard_map/reduce_scatter | solution.py:69
  124.5 5.0 %copy-start.5 = (bf16[1,128,2048]{2,1,0:T(8,128)(2,1)S(1)}, bf16[1,128,2048]{2,1,0:T(8,128)(2,1)}, u32[]{:S(2)}) copy-start(bf16[1,128,2048]{2,1,0:T(8,128)(2,1)} %copy-done.4) | copy-start | bytes 1572868
  124.5 5.0 %copy-start.19 = (bf16[128,768]{1,0:T(8,128)(2,1)S(1)}, bf16[128,768]{1,0:T(8,128)(2,1)}, u32[]{:S(2)}) copy-start(bf16[128,768]{1,0:T(8,128)(2,1)} %copy-done.18) | copy-start | bytes 589828
  129.4 3.8 %copy-start.17 = (bf16[128,768]{1,0:T(8,128)(2,1)S(1)}, bf16[128,768]{1,0:T(8,128)(2,1)}, u32[]{:S(2)}) copy-start(bf16[128,768]{1,0:T(8,128)(2,1)} %copy-done.16) | copy-start | bytes 589828
  129.4 99.2 %reduce-scatter.14.cloned.1.call-start = ((), (), s32[]{:S(2)}) async-start(), calls=%async_computation.9 | async-start | bytes 589824 | tf_op jit(solution)/shard_map/reduce_scatter | solution.py:101
  133.2 14.7 %copy-start.39 = (f32[16]{0:T(128)S(1)}, f32[16]{0:T(128)}, u32[]{:S(2)}) copy-start(f32[16]{0:T(128)} %copy-done.38) | copy-start | bytes 196
  133.2 44.4 %copy-start.23 = (bf16[1,16,2048]{2,1,0:T(8,128)(2,1)S(1)}, bf16[1,16,2048]{2,1,0:T(8,128)(2,1)}, u32[]{:S(2)}) copy-start(bf16[1,16,2048]{2,1,0:T(8,128)(2,1)} %param.25) | copy-start | bytes 196612
  133.2 62.6 %copy-start.11 = (bf16[2,128,2048]{2,1,0:T(8,128)(2,1)S(1)}, bf16[2,128,2048]{2,1,0:T(8,128)(2,1)}, u32[]{:S(2)}) copy-start(bf16[2,128,2048]{2,1,0:T(8,128)(2,1)} %param.21) | copy-start | bytes 3145732
  136.9 60.4 %copy-start.21 = (f32[1,1,2,128,128]{3,4,2,1,0:T(8,128)S(1)}, f32[1,1,2,128,128]{3,4,2,1,0:T(8,128)}, u32[]{:S(2)}) copy-start(f32[1,1,2,128,128]{3,4,2,1,0:T(8,128)} %copy-done.20) | copy-start | bytes 393220
  136.9 65.0 %copy-start.9 = (bf16[2048,2,128]{0,2,1:T(8,128)(2,1)S(1)}, bf16[2048,2,128]{0,2,1:T(8,128)(2,1)}, u32[]{:S(2)}) copy-start(bf16[2048,2,128]{0,2,1:T(8,128)(2,1)} %copy.41) | copy-start | bytes 3145732
  195.8 6.5 %copy-start.13 = (bf16[2048,1,128]{2,0,1:T(8,128)(2,1)S(1)}, bf16[2048,1,128]{2,0,1:T(8,128)(2,1)}, u32[]{:S(2)}) copy-start(bf16[2048,1,128]{2,0,1:T(8,128)(2,1)} %param.19) | copy-start | bytes 1572868
  197.4 5.2 %copy-start.14 = (bf16[2048,1,128]{2,0,1:T(8,128)(2,1)S(1)}, bf16[2048,1,128]{2,0,1:T(8,128)(2,1)}, u32[]{:S(2)}) copy-start(bf16[2048,1,128]{2,0,1:T(8,128)(2,1)} %param.20) | copy-start | bytes 1572868
  202.3 1.5 copy-start.3
  204.3 11.2 %copy-start.25 = (bf16[128,2,128]{0,2,1:T(8,128)(2,1)S(1)}, bf16[128,2,128]{0,2,1:T(8,128)(2,1)}, u32[]{:S(2)}) copy-start(bf16[128,2,128]{0,2,1:T(8,128)(2,1)} %copy-done.24) | copy-start | bytes 196612
  212.9 15.7 %copy-start.35 = (f32[16]{0:T(128)S(1)}, f32[16]{0:T(128)}, u32[]{:S(2)}) copy-start(f32[16]{0:T(128)} %copy-done.34) | copy-start | bytes 196
  212.9 16.8 %copy-start.33 = (f32[2048]{0:T(1024)S(1)}, f32[2048]{0:T(1024)}, u32[]{:S(2)}) copy-start(f32[2048]{0:T(1024)} %get-tuple-element.35) | copy-start | bytes 24580
  271.5 9.9 %copy-start.1 = (bf16[768,2048]{1,0:T(8,128)(2,1)S(1)}, bf16[768,2048]{1,0:T(8,128)(2,1)}, u32[]{:S(2)}) copy-start(bf16[768,2048]{1,0:T(8,128)(2,1)} %param.24) | copy-start | bytes 9437188
Sparse Core Ops, SparseCore 0:
  17.6 29.5 reduce-scatter.5
  71.9 24.6 reduce-scatter.7
  123.2 24.6 reduce-scatter.11
  150.6 26.9 reduce-scatter.9
  203.9 24.5 reduce-scatter.13
where the time goes:
time: 289 us; the launch traced here: 288 us
  blocking collectives  103 us (36%)
  waiting for transfers between devices  88 us (30%)
  matrix products  37.1 us (13%)
  other arithmetic  23.8 us (8%)
  local copies, waits for them, and re-layouts  21.2 us (7%)
  between operations  14.4 us (5%)
    reduce_scatter x1, waiting for transfers between devices, layer_pass(): mlp_sum = lax.psum_scatter(mlp_part, 'tp', scatter_dimension=1, tiled=True)  28.2 us
    reduce_scatter x1, waiting for transfers between devices, device_fn(): lax.psum_scatter(partial_emb, 'tp', scatter_dimension=1, tiled=True)  25.7 us
    psum x1, blocking collectives, layer_pass(): gain_grads = lax.psum(jnp.stack([gain_attn_part, gain_mlp_part]), 'tp')  23.5 us
    all_gather x1, blocking collectives, device_fn(): grad_first_full = lax.all_gather(grad_first, 'tp', axis=1, tiled=True)  16.8 us
    all_gather x1, blocking collectives, layer_pass(): grad_h1_full = lax.all_gather(grad_h1, 'tp', axis=1, tiled=True)  16.6 us
    all_gather x1, blocking collectives, layer_pass(): gathered2 = lax.all_gather(normed2_bf, 'tp', axis=1, tiled=True)  16.5 us
    all_gather x1, blocking collectives, layer_pass(): gathered1 = lax.all_gather(normed1_bf, 'tp', axis=1, tiled=True)  16.5 us
    unnamed x88, local copies, waits for them, and re-layouts  13.9 us
  transfers between devices with their start and end apart: 5, of which 5 were waited for; matrix products, arithmetic and copies ran while one was open for 11% of the time, Pallas kernels for 0%

commit v1 on v0

v1 whole, which is shorter than its diff:
```python
import functools

import jax
import jax.numpy as jnp
import numpy as np
from jax import lax
from jax.experimental import pallas as pl
from jax.experimental.pallas import tpu as pltpu
from jax.sharding import PartitionSpec as P

ROPE_THETA = 1000000.0
RMS_EPS = 1e-5
MESH = pl.DeviceIdType.MESH
BF = jnp.bfloat16
F32 = jnp.float32
NT = (((1,), (1,)), ((), ()))
TN = (((0,), (0,)), ((), ()))

N1, GH, N2, GH1, GF, GAIN = range(6)
R_EMB, R_ATT, R_GN2, R_MLP, R_GN1 = range(5)
RS_CHUNKS = {R_EMB: 4, R_ATT: 2, R_GN2: 4, R_MLP: 2, R_GN1: 2}


def dot(a, b, dims=(((1,), (0,)), ((), ()))):
    return lax.dot_general(a, b, dims, preferred_element_type=F32)


def layer_kernel(n_tp, local_heads,
                 tok, pos, invf, ga, gm, gh_in, emb, wq4, wk, wv, wo, wg, wu, wd,
                 o_n1, o_n2, o_gh, o_gh1, o_gf, o_act, o_gcat, o_heads, o_gqkv, o_gain, o_hid,
                 embv, onehot, wqr, wqf, wqkv, wov, wguv, wdv, ag, pb, rd, sb, rr,
                 act, gcat, heads, gqkv, gbuf, hid, x0f, nrm1, nrm2, h1f, gh1f, inv, gact, qkvb, tabs, probs,
                 ag_s, ag_r, rs_s, rs_r, loc):
    chips = n_tp // 2
    seq = tok.shape[1]
    rows, dim = emb.shape
    ffn = wd.shape[0]
    blk = gh_in.shape[0]
    hd = wk.shape[1]
    scale = hd ** -0.5
    qw = local_heads * hd

    me = lax.axis_index('tp')
    chip = me // 2
    core = lax.rem(me, 2)
    sib = 2 * chip + 1 - core

    def peer_chip(d):
        return lax.rem(chip + d, chips)

    def peer(d):
        return 2 * peer_chip(d) + core

    order = sorted(range(1, chips), key=lambda d: -min(d, chips - d))

    barrier = pltpu.get_barrier_semaphore()
    for dev in [sib] + [peer(d) for d in range(1, chips)]:
        pl.semaphore_signal(barrier, inc=1, device_id={'tp': dev}, device_id_type=MESH)

    pending = []
    nloc = [0]

    def local(src, dst):
        cp = pltpu.make_async_copy(src, dst, loc.at[nloc[0]])
        nloc[0] += 1
        cp.start()
        return cp

    n_emb = RS_CHUNKS[R_EMB]
    ew = dim // n_emb
    emb_cp = [local(emb.at[:, pl.ds(j * ew, ew)], embv.at[:, pl.ds(j * ew, ew)]) for j in range(n_emb)]

    tok_t = jnp.transpose(jnp.broadcast_to(tok[...].astype(F32), (seq, seq)))
    tok_t = tok_t - (me * rows).astype(F32)
    lane = lax.broadcasted_iota(jnp.int32, (seq, seq), 1).astype(F32)
    for b in range(rows // seq):
        onehot[:, b * seq:(b + 1) * seq] = jnp.where(tok_t == lane + float(b * seq), 1.0, 0.0).astype(BF)

    def remote(src, dst, s, r, dev):
        return pltpu.make_async_remote_copy(src_ref=src, dst_ref=dst, send_sem=s, recv_sem=r,
                                            device_id={'tp': dev}, device_id_type=MESH)

    def send(*args):
        cp = remote(*args)
        cp.start()
        pending.append(cp)

    def ag_ref(p, t):
        return gbuf.at[t] if p == GAIN else ag.at[p, t]

    def ag_start(p):
        mine = ag_ref(p, me)
        for d in order:
            send(mine, mine, ag_s.at[p, d], ag_r.at[p, d], peer(d))
        send(mine, mine, ag_s.at[p, 0], ag_r.at[p, 0], sib)

    def ag_finish(p):
        for d in sorted(range(1, chips), key=lambda d: min(d, chips - d)):
            src = lax.rem(chip + chips - d, chips)
            got = ag_ref(p, 2 * src + core)
            remote(got, got, ag_s.at[p, d], ag_r.at[p, d], sib).wait_recv()
            send(got, got, ag_s.at[p, chips - 1 + d], ag_r.at[p, chips - 1 + d], sib)
        got = ag_ref(p, sib)
        remote(got, got, ag_s.at[p, 0], ag_r.at[p, 0], sib).wait_recv()
        for d in sorted(range(1, chips), key=lambda d: min(d, chips - d)):
            src = lax.rem(chip + chips - d, chips)
            got = ag_ref(p, 2 * src + 1 - core)
            remote(got, got, ag_s.at[p, chips - 1 + d], ag_r.at[p, chips - 1 + d], sib).wait_recv()

    def gathered(p):
        return ag[p].reshape(seq, dim)

    def rs_cols(p, j):
        w = dim // RS_CHUNKS[p]
        return slice(j * w, (j + 1) * w)

    def rs_local(p, j, val):
        c = rs_cols(p, j)
        w = c.stop - c.start
        pb[p, :, :, :, c] = val.astype(BF).reshape(chips, 2, blk, w)
        send(pb.at[p, :, 1 - core, :, c], rd.at[p, :, :, c], rs_s.at[p, j, 0], rs_r.at[p, j, 0], sib)

    def rs_cross(p, j):
        c = rs_cols(p, j)
        remote(rd.at[p, :, :, c], rd.at[p, :, :, c], rs_s.at[p, j, 0], rs_r.at[p, j, 0], sib).wait_recv()
        for d in order:
            to = peer_chip(d)
            both = pb[p, to, core, :, c].astype(F32) + rd[p, to, :, c].astype(F32)
            sb[p, to, :, c] = both.astype(BF)
            send(sb.at[p, to, :, c], rr.at[p, d - 1, :, c], rs_s.at[p, j, d], rs_r.at[p, j, d], peer(d))

    def rs_finish(p):
        parts = []
        for j in range(RS_CHUNKS[p]):
            c = rs_cols(p, j)
            total = pb[p, chip, core, :, c].astype(F32) + rd[p, chip, :, c].astype(F32)
            for d in order[::-1]:
                remote(rr.at[p, d - 1, :, c], rr.at[p, d - 1, :, c], rs_s.at[p, j, d], rs_r.at[p, j, d], sib).wait_recv()
                total = total + rr[p, d - 1, :, c].astype(F32)
            parts.append(total)
        return jnp.concatenate(parts, axis=1)

    def rs_start(p, chunk):
        for j in range(RS_CHUNKS[p] + 1):
            if j < RS_CHUNKS[p]:
                rs_local(p, j, chunk(rs_cols(p, j)))
            if j > 0:
                rs_cross(p, j - 1)

    def norm_fwd(x, gain):
        r = lax.rsqrt(jnp.mean(x * x, axis=-1, keepdims=True) + RMS_EPS)
        n = x * r
        return (n * gain).astype(BF), n, r

    def norm_bwd(g, n, r, gain):
        part = jnp.sum(g * n, axis=0, keepdims=True)
        scaled = g * gain
        return r * (scaled - n * jnp.mean(scaled * n, axis=-1, keepdims=True)), part

    pl.semaphore_wait(barrier, chips)

    w_cp = {}

    def emb_chunk(c):
        j = c.start // ew
        emb_cp[j].wait()
        if j == n_emb - 2:
            w_cp['k'] = local(wk, wqkv.at[:, pl.ds(qw, hd)])
            w_cp['v'] = local(wv, wqkv.at[:, pl.ds(qw + hd, hd)])
            w_cp['q'] = local(wq4, wqr)
            w_cp['o'] = local(wo, wov)
        if j == n_emb - 1:
            w_cp['d'] = local(wd, wdv)
            w_cp['g'] = local(wg, wguv.at[:, pl.ds(0, ffn)])
            w_cp['u'] = local(wu, wguv.at[:, pl.ds(ffn, ffn)])
        return dot(onehot[...], embv[:, c])

    rs_start(R_EMB, emb_chunk)

    pos_t = jnp.transpose(jnp.broadcast_to(pos[...].astype(F32), (seq, seq)))
    angle = pos_t * invf[...]
    half = lax.broadcasted_iota(jnp.int32, (seq, hd), 1) < hd // 2
    tabs[0] = jnp.cos(angle)
    sin = jnp.sin(angle)
    tabs[1] = jnp.where(half, -sin, sin)
    w_cp['q'].wait()
    wqf[...] = wqr[...].astype(F32)
    for h in range(local_heads):
        wqkv[:, h * hd:(h + 1) * hd] = wqf[pl.ds(h, dim, stride=local_heads), :].astype(BF)

    x0 = rs_finish(R_EMB)
    x0f[...] = x0
    n1b, n1, r1 = norm_fwd(x0, ga[...])
    ag[N1, me] = n1b
    nrm1[...] = n1
    inv[0] = jnp.broadcast_to(r1, (blk, hd))
    ag_start(N1)
    ag[GH, me] = gh_in[...]
    ag_start(GH)
    w_cp['k'].wait()
    w_cp['v'].wait()
    ag_finish(N1)
    outs = [local(ag.at[N1], o_n1)]

    def rotate(v, sign):
        return v * tabs[0] + sign * (pltpu.roll(v, hd // 2, 1) * tabs[1])

    qkv = dot(gathered(N1), wqkv[...])
    for h in range(local_heads + 1):
        qkvb[:, h * hd:(h + 1) * hd] = rotate(qkv[:, h * hd:(h + 1) * hd], 1.0).astype(BF)
    qkvb[:, qw + hd:] = qkv[:, qw + hd:].astype(BF)
    kb = qkvb[:, qw:qw + hd]
    vb = qkvb[:, qw + hd:]
    causal = lax.broadcasted_iota(jnp.int32, (seq, seq), 0) >= lax.broadcasted_iota(jnp.int32, (seq, seq), 1)
    for h in range(local_heads):
        s = dot(qkvb[:, h * hd:(h + 1) * hd], kb, NT) * scale
        s = jnp.where(causal, s, -1e30)
        e = jnp.exp(s - jnp.max(s, axis=-1, keepdims=True))
        pr = e / jnp.sum(e, axis=-1, keepdims=True)
        probs[h] = pr
        heads[:, h * hd:(h + 1) * hd] = dot(pr.astype(BF), vb).astype(BF)
    w_cp['o'].wait()
    rs_start(R_ATT, lambda c: dot(heads[...], wov[:, c]))
    outs.append(local(heads, o_heads))

    ag_finish(GH)
    outs.append(local(ag.at[GH], o_gh))
    w_cp['d'].wait()
    gact[...] = dot(gathered(GH), wdv[...], NT).astype(BF).astype(F32)

    h1 = (x0f[...] + rs_finish(R_ATT).astype(BF).astype(F32)).astype(BF).astype(F32)
    h1f[...] = h1
    n2b, n2, r2 = norm_fwd(h1, gm[...])
    ag[N2, me] = n2b
    nrm2[...] = n2
    inv[1] = jnp.broadcast_to(r2, (blk, hd))
    ag_start(N2)
    w_cp['g'].wait()
    w_cp['u'].wait()
    ag_finish(N2)
    outs.append(local(ag.at[N2], o_n2))

    fw = 256
    for j in range(ffn // fw):
        c = slice(j * fw, (j + 1) * fw)
        cu = slice(ffn + j * fw, ffn + (j + 1) * fw)
        gate = dot(gathered(N2), wguv[:, c])
        up = dot(gathered(N2), wguv[:, cu])
        sig = jax.nn.sigmoid(gate)
        ga_act = gate * sig
        act[:, c] = (ga_act * up).astype(BF)
        g = gact[:, c]
        gcat[:, cu] = (g * ga_act).astype(BF)
        gcat[:, c] = (g * up * sig * (1.0 + gate * (1.0 - sig))).astype(BF)
    rs_start(R_GN2, lambda c: dot(gcat[...], wguv[c, :], NT))
    outs.append(local(gcat, o_gcat))
    outs.append(local(act, o_act))
    for j in range(RS_CHUNKS[R_MLP]):
        rs_local(R_MLP, j, dot(act[...], wdv[:, rs_cols(R_MLP, j)]))

    gn2 = rs_finish(R_GN2).astype(BF).astype(F32)
    g_in, gain_part = norm_bwd(gn2, nrm2[...], inv[1][:, :1], gm[...])
    gbuf[me, 1:2, :] = gain_part
    gh1 = (gh_in[...].astype(F32) + g_in).astype(BF)
    gh1f[...] = gh1.astype(F32)
    ag[GH1, me] = gh1
    ag_start(GH1)
    for j in range(RS_CHUNKS[R_MLP]):
        rs_cross(R_MLP, j)
    ag_finish(GH1)
    outs.append(local(ag.at[GH1], o_gh1))

    ghd = dot(gathered(GH1), wov[...], NT).astype(BF)
    gv = jnp.zeros((seq, hd), F32)
    gk = jnp.zeros((seq, hd), F32)
    for h in range(local_heads):
        g = ghd[:, h * hd:(h + 1) * hd]
        pr = probs[h]
        gp = dot(g, vb, NT).astype(BF).astype(F32)
        gv = gv + dot(pr.astype(BF), g, TN)
        gs = (pr * (gp - jnp.sum(gp * pr, axis=-1, keepdims=True)) * scale).astype(BF)
        gq = dot(gs, kb).astype(BF).astype(F32)
        gk = gk + dot(gs, qkvb[:, h * hd:(h + 1) * hd], TN)
        gqkv[:, h * hd:(h + 1) * hd] = rotate(gq, -1.0).astype(BF)
    gqkv[:, qw:qw + hd] = rotate(gk.astype(BF).astype(F32), -1.0).astype(BF)
    gqkv[:, qw + hd:] = gv.astype(BF)
    rs_start(R_GN1, lambda c: dot(gqkv[...], wqkv[c, :], NT))
    outs.append(local(gqkv, o_gqkv))
    hid[...] = (h1f[...] + rs_finish(R_MLP).astype(BF).astype(F32)).astype(BF)
    outs.append(local(hid, o_hid))

    gn1 = rs_finish(R_GN1).astype(BF).astype(F32)
    g_in, gain_part = norm_bwd(gn1, nrm1[...], inv[0][:, :1], ga[...])
    gbuf[me, 0:1, :] = gain_part
    ag[GF, me] = (gh1f[...] + g_in).astype(BF)
    ag_start(GF)
    ag_start(GAIN)
    ag_finish(GF)
    outs.append(local(ag.at[GF], o_gf))
    ag_finish(GAIN)
    outs.append(local(gbuf, o_gain))
    for cp in pending:
        cp.wait_send()
    for cp in outs:
        cp.wait()


def grads_kernel(n_tp, local_heads,
                 tok, n1, n2, gh, gh1, gf, act, gcat, heads, gqkv, gain, hid,
                 o_hid, o_emb, o_wq, o_wk, o_wv, o_wo, o_wg, o_wu, o_wd, o_ga, o_gm,
                 wide, tall, qbuf, kvbuf, s_wide, s_tall, s_qkv):
    seq, dim = n1.shape
    rows = o_emb.shape[0]
    ffn = act.shape[1]
    hd = gqkv.shape[1] // (local_heads + 2)
    me = lax.axis_index('tp')
    n_wide, wr = wide.shape[0], wide.shape[1]
    n_tall, tr = tall.shape[0], tall.shape[1]
    busy = {}

    def put(key, src, dst, sem):
        cp = pltpu.make_async_copy(src, dst, sem)
        cp.start()
        busy[key] = cp

    def free(key):
        if key in busy:
            busy.pop(key).wait()

    tok_l = tok[...] - me * rows
    row = lax.broadcasted_iota(jnp.int32, (wr, seq), 0)
    wide_units = []
    for u in range(act.shape[1] // wr):
        wide_units.append((lambda u=u: dot(act[:, u * wr:(u + 1) * wr], gh[...], TN), o_wd.at[pl.ds(u * wr, wr)]))
    for u in range(heads.shape[1] // wr):
        wide_units.append((lambda u=u: dot(heads[:, u * wr:(u + 1) * wr], gh1[...], TN), o_wo.at[pl.ds(u * wr, wr)]))
    for u in range(rows // wr):
        wide_units.append((lambda u=u: dot(jnp.where(row + u * wr == tok_l, 1.0, 0.0).astype(BF), gf[...]), o_emb.at[pl.ds(u * wr, wr)]))
    tall_units = []
    for half, out in ((0, o_wg), (1, o_wu)):
        for u in range(dim // tr):
            tall_units.append((lambda u=u, half=half: dot(n2[:, u * tr:(u + 1) * tr], gcat[:, half * ffn:(half + 1) * ffn], TN),
                               out.at[pl.ds(u * tr, tr)]))
    iw = it = 0
    while iw < len(wide_units) or it < len(tall_units):
        if it < len(tall_units):
            slot = it % n_tall
            free(('t', slot))
            tall[slot] = tall_units[it][0]()
            put(('t', slot), tall.at[slot], tall_units[it][1], s_tall.at[slot])
            it += 1
        if iw < len(wide_units):
            slot = iw % n_wide
            free(('w', slot))
            wide[slot] = wide_units[iw][0]()
            put(('w', slot), wide.at[slot], wide_units[iw][1], s_wide.at[slot])
            iw += 1
    qw = local_heads * hd
    for i, out in enumerate((o_wk, o_wv)):
        kvbuf[i] = dot(n1[...], gqkv[:, qw + i * hd:qw + (i + 1) * hd], TN)
        put(('k', i), kvbuf.at[i], out, s_qkv.at[i])
    for h in range(local_heads):
        qbuf[pl.ds(h, dim, stride=local_heads), :] = dot(n1[...], gqkv[:, h * hd:(h + 1) * hd], TN)
    put(('q', 0), qbuf, o_wq, s_qkv.at[2])

    o_hid[...] = hid[...]
    total = gain[0]
    for t in range(1, n_tp):
        total = total + gain[t]
    o_ga[...] = total[0:1]
    o_gm[...] = total[1:2]
    for key in list(busy):
        free(key)


def solution(mesh):
    n_tp = mesh.shape['tp']
    chips = n_tp // 2
    in_specs = (P('dp', None), P('dp', None), P('tp', None), P(None), P(None),
                P(None, 'tp', None), P(None, 'tp', None), P(None, 'tp', None), P('tp', None, None),
                P(None, 'tp'), P(None, 'tp'), P('tp', None), P('dp', 'tp', None))
    out_specs = (P('dp', 'tp', None), P(('dp', 'tp'), None),
                 P('dp', 'tp', None), P('dp', 'tp', None), P('dp', 'tp', None), P(('dp', 'tp'), None, None),
                 P('dp', 'tp'), P('dp', 'tp'), P(('dp', 'tp'), None), P('dp'), P('dp'))

    def device_fn(tokens, positions, emb, gain_attn, gain_mlp, w_query, w_key, w_value, w_out, w_gate, w_up, w_down, grad_hidden):
        seq = tokens.shape[1]
        rows, dim = emb.shape
        lh, hd = w_query.shape[1], w_query.shape[2]
        ffn = w_down.shape[0]
        blk = grad_hidden.shape[1]
        qkvw = (lh + 2) * hd
        inv_freq = (np.float32(ROPE_THETA) ** (-np.arange(hd // 2, dtype=np.float32) * np.float32(2.0 / hd))).astype(np.float32)
        invf = jnp.asarray(np.concatenate([inv_freq, inv_freq])[None, :])

        def sds(shape, dt=BF):
            return jax.ShapeDtypeStruct(shape, dt)

        vm = pl.BlockSpec(memory_space=pltpu.VMEM)
        hb = pl.BlockSpec(memory_space=pl.ANY)
        maxc = max(RS_CHUNKS.values())
        mid = pl.pallas_call(
            functools.partial(layer_kernel, n_tp, lh),
            name='layer',
            out_shape=[sds((n_tp, blk, dim))] * 5 + [sds((seq, ffn)), sds((seq, 2 * ffn)), sds((seq, lh * hd)), sds((seq, qkvw)),
                                                    sds((n_tp, 2, dim), F32), sds((blk, dim))],
            in_specs=[vm] * 6 + [hb] * 8,
            out_specs=[hb] * 11,
            scratch_shapes=[
                pltpu.VMEM((rows, dim), BF), pltpu.VMEM((seq, rows), BF), pltpu.VMEM((dim * lh, hd), BF), pltpu.VMEM((dim * lh, hd), F32),
                pltpu.VMEM((dim, qkvw), BF), pltpu.VMEM((lh * hd, dim), BF), pltpu.VMEM((dim, 2 * ffn), BF), pltpu.VMEM((ffn, dim), BF),
                pltpu.VMEM((5, n_tp, blk, dim), BF), pltpu.VMEM((5, chips, 2, blk, dim), BF), pltpu.VMEM((5, chips, blk, dim), BF),
                pltpu.VMEM((5, chips, blk, dim), BF), pltpu.VMEM((5, chips - 1, blk, dim), BF),
                pltpu.VMEM((seq, ffn), BF), pltpu.VMEM((seq, 2 * ffn), BF), pltpu.VMEM((seq, lh * hd), BF), pltpu.VMEM((seq, qkvw), BF),
                pltpu.VMEM((n_tp, 2, dim), F32), pltpu.VMEM((blk, dim), BF),
                pltpu.VMEM((blk, dim), F32), pltpu.VMEM((blk, dim), F32), pltpu.VMEM((blk, dim), F32), pltpu.VMEM((blk, dim), F32),
                pltpu.VMEM((blk, dim), F32), pltpu.VMEM((2, blk, hd), F32), pltpu.VMEM((seq, ffn), F32), pltpu.VMEM((seq, qkvw), BF),
                pltpu.VMEM((2, seq, hd), F32), pltpu.VMEM((lh, seq, seq), F32),
                pltpu.SemaphoreType.DMA((6, 2 * chips - 1)), pltpu.SemaphoreType.DMA((6, 2 * chips - 1)),
                pltpu.SemaphoreType.DMA((5, maxc, chips)), pltpu.SemaphoreType.DMA((5, maxc, chips)),
                pltpu.SemaphoreType.DMA((32,)),
            ],
            compiler_params=pltpu.CompilerParams(collective_id=0, has_side_effects=True, vmem_limit_bytes=64 * 1024 * 1024 - 65536),
        )(tokens, positions, invf, gain_attn.reshape(1, dim), gain_mlp.reshape(1, dim), grad_hidden.reshape(blk, dim),
          emb, w_query.reshape(dim * lh, hd), w_key.reshape(dim, hd), w_value.reshape(dim, hd), w_out.reshape(lh * hd, dim),
          w_gate, w_up, w_down)
        n1, n2, gh, gh1, gf, act, gcat, heads, gqkv, gain, hid = mid
        n1, n2, gh, gh1, gf = (a.reshape(seq, dim) for a in (n1, n2, gh, gh1, gf))
        wide_rows, tall_rows = 256, 512
        res = pl.pallas_call(
            functools.partial(grads_kernel, n_tp, lh),
            name='grads',
            out_shape=[sds((blk, dim)), sds((rows, dim), F32), sds((dim * lh, hd), F32), sds((dim, hd), F32), sds((dim, hd), F32),
                       sds((lh * hd, dim), F32), sds((dim, ffn), F32), sds((dim, ffn), F32), sds((ffn, dim), F32),
                       sds((1, dim), F32), sds((1, dim), F32)],
            in_specs=[vm] * 12,
            out_specs=[vm] + [hb] * 8 + [vm] * 2,
            scratch_shapes=[
                pltpu.VMEM((3, wide_rows, dim), F32), pltpu.VMEM((3, tall_rows, ffn), F32), pltpu.VMEM((dim * lh, hd), F32),
                pltpu.VMEM((2, dim, hd), F32),
                pltpu.SemaphoreType.DMA((3,)), pltpu.SemaphoreType.DMA((3,)), pltpu.SemaphoreType.DMA((3,)),
            ],
            compiler_params=pltpu.CompilerParams(vmem_limit_bytes=60 * 1024 * 1024),
        )(tokens, n1, n2, gh, gh1, gf, act, gcat, heads, gqkv, gain, hid)
        o_hid, o_emb, o_wq, o_wk, o_wv, o_wo, o_wg, o_wu, o_wd, o_ga, o_gm = res
        return (o_hid.reshape(1, blk, dim), o_emb, o_wq.reshape(dim, lh, hd), o_wk.reshape(dim, 1, hd), o_wv.reshape(dim, 1, hd),
                o_wo.reshape(lh, hd, dim), o_wg, o_wu, o_wd, o_ga.reshape(dim), o_gm.reshape(dim))

    return jax.shard_map(device_fn, mesh=mesh, in_specs=in_specs, out_specs=out_specs, check_vma=False)
```

time: 289 us -> 83.4 us (0.29)
  blocking collectives: 103 us -> 0 us
  waiting for transfers between devices: 88 us -> 0 us
  Pallas kernels: 0 us -> 82.4 us
  matrix products: 37.1 us -> 0 us
  other arithmetic: 23.8 us -> 0 us
  local copies, waits for them, and re-layouts: 21.2 us -> 0 us
  between operations: 14.4 us -> 0.82 us
    reduce_scatter x5 -> x0, waiting for transfers between devices: 87.8 us -> none  [the longest x1 28.2 us: layer_pass(): mlp_sum = lax.psum_scatter(mlp_part, 'tp', scatter_dimension=1, tiled=True)]
    pallas_call x0 -> x2, Pallas kernels: none -> 82.4 us  [the longest x1 65.8 us: device_fn(): pl.pallas_call(functools.partial(layer_kernel, n_tp, lh), name='layer', o...]
    all_gather x5 -> x0, blocking collectives: 79.6 us -> none  [the longest x1 16.8 us: device_fn(): grad_first_full = lax.all_gather(grad_first, 'tp', axis=1, tiled=True)]
    dot_general x26 -> x0, matrix products: 36.7 us -> none  [the longest x1 4.81 us: layer_pass(): jnp.einsum('bsf,bsd->fd', act_bf, grad_full, preferred_element_type=jnp.f...]
    psum x1 -> x0, blocking collectives: 23.5 us -> none  [layer_pass(): gain_grads = lax.psum(jnp.stack([gain_attn_part, gain_mlp_part]), 'tp')]
    unnamed x88 -> x0, local copies, waits for them, and re-layouts: 13.9 us -> none
    scatter-add x1 -> x0, other arithmetic: 9.91 us -> none  [device_fn(): jax.ops.segment_sum(grad_first_full.reshape(-1, grad_first_full.shape[-1]...]
    gather x1 -> x0, local copies, waits for them, and re-layouts: 6.7 us -> none  [device_fn(): jnp.take(emb_shard, jnp.clip(local_ids, 0, rows_local - 1), axis=0)]
  transfers between devices with their start and end apart: 5 -> 0, of which waited for: 5 -> 0; matrix products, arithmetic and copies ran while one was open for 11% -> 0% of each run, Pallas kernels for 0% -> 0%
where the time goes in v1:
time: 83.4 us; the launch traced here: 83.2 us
  Pallas kernels  82.4 us (99%)
    pallas_call x1, Pallas kernels, device_fn(): pl.pallas_call(functools.partial(layer_kernel, n_tp, lh), name='layer', o...  65.8 us
    pallas_call x1, Pallas kernels, device_fn(): pl.pallas_call(functools.partial(grads_kernel, n_tp, lh), name='grads', o...  16.6 us

profile of v1, /device:TPU:81, one launch (start us, length us, event | category | flops | bytes accessed | tf_op | source)
XLA Modules:
  0.0 83.2 jit_solution(13830209993821379516)
XLA Ops:
  0.6 65.8 %layer.1 = (bf16[8,16,2048]{2,1,0:T(8,128)(2,1)}, bf16[8,16,2048]{2,1,0:T(8,128)(2,1)}, bf16[8,16,2048]{2,1,0:T(8,128)(2,1)}, bf16[8,16,2048]{2,1,0:T(8,128)(2,1...) custom-call(s32[1,128]{1,0:T(1,128)} %tok.3, ...), custom_call_target="tpu_custom_call" | custom-call | tf_op jit(solution)/shard_map/layer/pallas_call | solution.py:402
  66.5 16.6 %grads.1 = (bf16[16,2048]{1,0:T(8,128)(2,1)}, f32[2048,2048]{1,0:T(8,128)}, f32[4096,128]{1,0:T(8,128)}, f32[2048,128]{1,0:T(8,128)}, f32[2048,128]{1,0:T(8,128)...) custom-call(s32[1,128]{1,0:T(1,128)} %tok.3, ...), custom_call_target="tpu_custom_call" | custom-call | tf_op jit(solution)/shard_map/grads/pallas_call | solution.py:430

commit v2 on v1

--- a/solution.py
+++ b/solution.py
@@ -25,14 +25,23 @@
     return lax.dot_general(a, b, dims, preferred_element_type=F32)
 
 
+def scoped(name):
+    def wrap(fn):
+        def run(p, *rest):
+            with jax.named_scope(f'{name}_{p}'):
+                return fn(p, *rest)
+        return run
+    return wrap
+
+
 def layer_kernel(n_tp, local_heads,
-                 tok, pos, invf, ga, gm, gh_in, emb, wq4, wk, wv, wo, wg, wu, wd,
+                 h_tok, h_pos, h_invf, h_ga, h_gm, h_gh, emb, wq4, wk, wv, wo, wg, wu, wd,
                  o_n1, o_n2, o_gh, o_gh1, o_gf, o_act, o_gcat, o_heads, o_gqkv, o_gain, o_hid,
-                 embv, onehot, wqr, wqf, wqkv, wov, wguv, wdv, ag, pb, rd, sb, rr,
+                 tok, pos, invf, ga, gm, gh_in, embv, onehot, wqr, wqf, wqkv, wov, wguv, wdv, ag, pb, rd, sb, rr,
                  act, gcat, heads, gqkv, gbuf, hid, x0f, nrm1, nrm2, h1f, gh1f, inv, gact, qkvb, tabs, probs,
                  ag_s, ag_r, rs_s, rs_r, loc):
     chips = n_tp // 2
-    seq = tok.shape[1]
+    seq = h_tok.shape[1]
     rows, dim = emb.shape
     ffn = wd.shape[0]
     blk = gh_in.shape[0]
@@ -57,18 +66,26 @@
     for dev in [sib] + [peer(d) for d in range(1, chips)]:
         pl.semaphore_signal(barrier, inc=1, device_id={'tp': dev}, device_id_type=MESH)
 
-    pending = []
-    nloc = [0]
-
-    def local(src, dst):
-        cp = pltpu.make_async_copy(src, dst, loc.at[nloc[0]])
-        nloc[0] += 1
+    nloc = [1]
+
+    def local(src, dst, slot=None):
+        if slot is None:
+            slot = nloc[0]
+            nloc[0] += 1
+        cp = pltpu.make_async_copy(src, dst, loc.at[slot])
         cp.start()
         return cp
 
     n_emb = RS_CHUNKS[R_EMB]
     ew = dim // n_emb
-    emb_cp = [local(emb.at[:, pl.ds(j * ew, ew)], embv.at[:, pl.ds(j * ew, ew)]) for j in range(n_emb)]
+
+    def emb_load(j):
+        return local(emb.at[:, pl.ds(j * ew, ew)], embv.at[:, pl.ds(j * ew, ew)])
+
+    in_cp = [local(h_tok, tok)]
+    emb_cp = [emb_load(0), emb_load(1)]
+    in_cp += [local(a, b) for a, b in ((h_pos, pos), (h_invf, invf), (h_ga, ga), (h_gm, gm), (h_gh, gh_in))]
+    in_cp[0].wait()
 
     tok_t = jnp.transpose(jnp.broadcast_to(tok[...].astype(F32), (seq, seq)))
     tok_t = tok_t - (me * rows).astype(F32)
@@ -81,71 +98,113 @@
                                             device_id={'tp': dev}, device_id_type=MESH)
 
     def send(*args):
-        cp = remote(*args)
-        cp.start()
-        pending.append(cp)
+        remote(*args).start()
+
+    near = sorted(range(1, chips), key=lambda d: min(d, chips - d))
+    incoming = [(d, c) for d in near for c in (1, 0)]
+
+    ag_set = {N1: 0, N2: 0, GH1: 0, GF: 0, GH: 1, GAIN: 1}
 
     def ag_ref(p, t):
         return gbuf.at[t] if p == GAIN else ag.at[p, t]
 
+    def ag_block(p, d, c):
+        return ag_ref(p, 2 * lax.rem(chip + chips - d, chips) + c)
+
+    def ag_wait_sends(p):
+        own = gbuf.at[pl.ds(0, chips)] if p == GAIN else ag.at[p, pl.ds(0, chips)]
+        passed = gbuf.at[pl.ds(0, n_tp - 2)] if p == GAIN else ag.at[p, pl.ds(0, n_tp - 2)]
+        remote(own, own, ag_s.at[ag_set[p], 0], ag_r.at[ag_set[p], 0], sib).wait_send()
+
+        @pl.when(core == 1)
+        def _():
+            remote(passed, passed, ag_s.at[ag_set[p], 1], ag_r.at[ag_set[p], 0], sib).wait_send()
+
+    @scoped('ag_start')
     def ag_start(p):
         mine = ag_ref(p, me)
+        q = ag_set[p]
         for d in order:
-            send(mine, mine, ag_s.at[p, d], ag_r.at[p, d], peer(d))
-        send(mine, mine, ag_s.at[p, 0], ag_r.at[p, 0], sib)
-
-    def ag_finish(p):
-        for d in sorted(range(1, chips), key=lambda d: min(d, chips - d)):
-            src = lax.rem(chip + chips - d, chips)
-            got = ag_ref(p, 2 * src + core)
-            remote(got, got, ag_s.at[p, d], ag_r.at[p, d], sib).wait_recv()
-            send(got, got, ag_s.at[p, chips - 1 + d], ag_r.at[p, chips - 1 + d], sib)
-        got = ag_ref(p, sib)
-        remote(got, got, ag_s.at[p, 0], ag_r.at[p, 0], sib).wait_recv()
-        for d in sorted(range(1, chips), key=lambda d: min(d, chips - d)):
-            src = lax.rem(chip + chips - d, chips)
-            got = ag_ref(p, 2 * src + 1 - core)
-            remote(got, got, ag_s.at[p, chips - 1 + d], ag_r.at[p, chips - 1 + d], sib).wait_recv()
+            send(mine, mine, ag_s.at[q, 0], ag_r.at[q, 2 * d - core], 2 * peer_chip(d) + 1)
+        send(mine, mine, ag_s.at[q, 0], ag_r.at[q, 0], sib)
+
+    @scoped('ag_finish')
+    def ag_finish(*ps):
+        @pl.when(core == 1)
+        def _():
+            for d, c in incoming:
+                for p in ps:
+                    got = ag_block(p, d, c)
+                    q = ag_set[p]
+                    remote(got, got, ag_s.at[q, 1], ag_r.at[q, 2 * d - c], sib).wait_recv()
+                    send(got, got, ag_s.at[q, 1], ag_r.at[q, 2 * d - c], sib)
+
+        for p in ps:
+            got = ag_ref(p, sib)
+            remote(got, got, ag_s.at[ag_set[p], 0], ag_r.at[ag_set[p], 0], sib).wait_recv()
+
+        @pl.when(core == 0)
+        def _():
+            for d, c in incoming:
+                for p in ps:
+                    got = ag_block(p, d, c)
+                    remote(got, got, ag_s.at[ag_set[p], 1], ag_r.at[ag_set[p], 2 * d - c], sib).wait_recv()
 
     def gathered(p):
         return ag[p].reshape(seq, dim)
+
+    rs_set = {R_EMB: 0, R_ATT: 0, R_GN2: 0, R_GN1: 0, R_MLP: 1}
+
+    def rs_wait_sends(p):
+        q = rs_set[p]
+        remote(rd.at[p], rd.at[p], rs_s.at[q, 0], rs_r.at[q, 0, 0], sib).wait_send()
+        remote(rr.at[p], rr.at[p], rs_s.at[q, 1], rs_r.at[q, 0, 0], sib).wait_send()
 
     def rs_cols(p, j):
         w = dim // RS_CHUNKS[p]
         return slice(j * w, (j + 1) * w)
 
+    @scoped('rs_local')
     def rs_local(p, j, val):
         c = rs_cols(p, j)
         w = c.stop - c.start
         pb[p, :, :, :, c] = val.astype(BF).reshape(chips, 2, blk, w)
-        send(pb.at[p, :, 1 - core, :, c], rd.at[p, :, :, c], rs_s.at[p, j, 0], rs_r.at[p, j, 0], sib)
-
+        send(pb.at[p, :, 1 - core, :, c], rd.at[p, :, :, c], rs_s.at[rs_set[p], 0], rs_r.at[rs_set[p], j, 0], sib)
+
+    @scoped('rs_cross')
     def rs_cross(p, j):
         c = rs_cols(p, j)
-        remote(rd.at[p, :, :, c], rd.at[p, :, :, c], rs_s.at[p, j, 0], rs_r.at[p, j, 0], sib).wait_recv()
+        remote(rd.at[p, :, :, c], rd.at[p, :, :, c], rs_s.at[rs_set[p], 0], rs_r.at[rs_set[p], j, 0], sib).wait_recv()
         for d in order:
             to = peer_chip(d)
             both = pb[p, to, core, :, c].astype(F32) + rd[p, to, :, c].astype(F32)
             sb[p, to, :, c] = both.astype(BF)
-            send(sb.at[p, to, :, c], rr.at[p, d - 1, :, c], rs_s.at[p, j, d], rs_r.at[p, j, d], peer(d))
-
+            send(sb.at[p, to, :, c], rr.at[p, d - 1, :, c], rs_s.at[rs_set[p], 1], rs_r.at[rs_set[p], j, d], peer(d))
+
+    @scoped('rs_finish')
     def rs_finish(p):
         parts = []
         for j in range(RS_CHUNKS[p]):
             c = rs_cols(p, j)
             total = pb[p, chip, core, :, c].astype(F32) + rd[p, chip, :, c].astype(F32)
             for d in order[::-1]:
-                remote(rr.at[p, d - 1, :, c], rr.at[p, d - 1, :, c], rs_s.at[p, j, d], rs_r.at[p, j, d], sib).wait_recv()
+                remote(rr.at[p, d - 1, :, c], rr.at[p, d - 1, :, c], rs_s.at[rs_set[p], 1], rs_r.at[rs_set[p], j, d], sib).wait_recv()
                 total = total + rr[p, d - 1, :, c].astype(F32)
             parts.append(total)
         return jnp.concatenate(parts, axis=1)
 
     def rs_start(p, chunk):
-        for j in range(RS_CHUNKS[p] + 1):
-            if j < RS_CHUNKS[p]:
-                rs_local(p, j, chunk(rs_cols(p, j)))
-            if j > 0:
-                rs_cross(p, j - 1)
+        n = RS_CHUNKS[p]
+        lag = 2 if n > 2 else 1
+        for j in range(n + lag):
+            if j < n:
+                val = chunk(rs_cols(p, j))
+                if p == R_EMB and j == 0:
+                    with jax.named_scope('barrier'):
+                        pl.semaphore_wait(barrier, chips)
+                rs_local(p, j, val)
+            if j >= lag:
+                rs_cross(p, j - lag)
 
     def norm_fwd(x, gain):
         r = lax.rsqrt(jnp.mean(x * x, axis=-1, keepdims=True) + RMS_EPS)
@@ -157,13 +216,13 @@
         scaled = g * gain
         return r * (scaled - n * jnp.mean(scaled * n, axis=-1, keepdims=True)), part
 
-    pl.semaphore_wait(barrier, chips)
-
     w_cp = {}
 
     def emb_chunk(c):
         j = c.start // ew
         emb_cp[j].wait()
+        if j + 2 < n_emb:
+            emb_cp.append(emb_load(j + 2))
         if j == n_emb - 2:
             w_cp['k'] = local(wk, wqkv.at[:, pl.ds(qw, hd)])
             w_cp['v'] = local(wv, wqkv.at[:, pl.ds(qw + hd, hd)])
@@ -177,6 +236,8 @@
 
     rs_start(R_EMB, emb_chunk)
 
+    in_cp[1].wait()
+    in_cp[2].wait()
     pos_t = jnp.transpose(jnp.broadcast_to(pos[...].astype(F32), (seq, seq)))
     angle = pos_t * invf[...]
     half = lax.broadcasted_iota(jnp.int32, (seq, hd), 1) < hd // 2
@@ -188,6 +249,8 @@
     for h in range(local_heads):
         wqkv[:, h * hd:(h + 1) * hd] = wqf[pl.ds(h, dim, stride=local_heads), :].astype(BF)
 
+    for cp in in_cp[3:]:
+        cp.wait()
     x0 = rs_finish(R_EMB)
     x0f[...] = x0
     n1b, n1, r1 = norm_fwd(x0, ga[...])
@@ -196,11 +259,12 @@
     inv[0] = jnp.broadcast_to(r1, (blk, hd))
     ag_start(N1)
     ag[GH, me] = gh_in[...]
-    ag_start(GH)
     w_cp['k'].wait()
     w_cp['v'].wait()
     ag_finish(N1)
-    outs = [local(ag.at[N1], o_n1)]
+    ag_start(GH)
+    outs = []
+    local(ag.at[N1], o_n1, 0)
 
     def rotate(v, sign):
         return v * tabs[0] + sign * (pltpu.roll(v, hd // 2, 1) * tabs[1])
@@ -220,13 +284,13 @@
         probs[h] = pr
         heads[:, h * hd:(h + 1) * hd] = dot(pr.astype(BF), vb).astype(BF)
     w_cp['o'].wait()
+    rs_wait_sends(R_EMB)
     rs_start(R_ATT, lambda c: dot(heads[...], wov[:, c]))
     outs.append(local(heads, o_heads))
 
     ag_finish(GH)
-    outs.append(local(ag.at[GH], o_gh))
+    local(ag.at[GH], o_gh, 0)
     w_cp['d'].wait()
-    gact[...] = dot(gathered(GH), wdv[...], NT).astype(BF).astype(F32)
 
     h1 = (x0f[...] + rs_finish(R_ATT).astype(BF).astype(F32)).astype(BF).astype(F32)
     h1f[...] = h1
@@ -234,11 +298,14 @@
     ag[N2, me] = n2b
     nrm2[...] = n2
     inv[1] = jnp.broadcast_to(r2, (blk, hd))
+    ag_wait_sends(N1)
     ag_start(N2)
+    with jax.named_scope('gact'):
+        gact[...] = dot(gathered(GH), wdv[...], NT).astype(BF).astype(F32)
     w_cp['g'].wait()
     w_cp['u'].wait()
     ag_finish(N2)
-    outs.append(local(ag.at[N2], o_n2))
+    local(ag.at[N2], o_n2, 0)
 
     fw = 256
     for j in range(ffn // fw):
@@ -252,6 +319,7 @@
         g = gact[:, c]
         gcat[:, cu] = (g * ga_act).astype(BF)
         gcat[:, c] = (g * up * sig * (1.0 + gate * (1.0 - sig))).astype(BF)
+    rs_wait_sends(R_ATT)
     rs_start(R_GN2, lambda c: dot(gcat[...], wguv[c, :], NT))
     outs.append(local(gcat, o_gcat))
     outs.append(local(act, o_act))
@@ -264,11 +332,12 @@
     gh1 = (gh_in[...].astype(F32) + g_in).astype(BF)
     gh1f[...] = gh1.astype(F32)
     ag[GH1, me] = gh1
+    ag_wait_sends(N2)
     ag_start(GH1)
+    ag_finish(GH1)
     for j in range(RS_CHUNKS[R_MLP]):
         rs_cross(R_MLP, j)
-    ag_finish(GH1)
-    outs.append(local(ag.at[GH1], o_gh1))
+    local(ag.at[GH1], o_gh1, 0)
 
     ghd = dot(gathered(GH1), wov[...], NT).astype(BF)
     gv = jnp.zeros((seq, hd), F32)
@@ -284,6 +353,7 @@
         gqkv[:, h * hd:(h + 1) * hd] = rotate(gq, -1.0).astype(BF)
     gqkv[:, qw:qw + hd] = rotate(gk.astype(BF).astype(F32), -1.0).astype(BF)
     gqkv[:, qw + hd:] = gv.astype(BF)
+    rs_wait_sends(R_GN2)
     rs_start(R_GN1, lambda c: dot(gqkv[...], wqkv[c, :], NT))
     outs.append(local(gqkv, o_gqkv))
     hid[...] = (h1f[...] + rs_finish(R_MLP).astype(BF).astype(F32)).astype(BF)
@@ -293,22 +363,29 @@
     g_in, gain_part = norm_bwd(gn1, nrm1[...], inv[0][:, :1], ga[...])
     gbuf[me, 0:1, :] = gain_part
     ag[GF, me] = (gh1f[...] + g_in).astype(BF)
+    ag_wait_sends(GH)
+    ag_wait_sends(GH1)
+    ag_start(GAIN)
     ag_start(GF)
-    ag_start(GAIN)
-    ag_finish(GF)
-    outs.append(local(ag.at[GF], o_gf))
-    ag_finish(GAIN)
+    ag_finish(GAIN, GF)
+    local(ag.at[GF], o_gf, 0)
     outs.append(local(gbuf, o_gain))
-    for cp in pending:
-        cp.wait_send()
-    for cp in outs:
-        cp.wait()
+    with jax.named_scope('tail_send'):
+        rs_wait_sends(R_GN1)
+        rs_wait_sends(R_MLP)
+        ag_wait_sends(GAIN)
+        ag_wait_sends(GF)
+
+    with jax.named_scope('tail_out'):
+        for cp in outs:
+            cp.wait()
+        pltpu.make_async_copy(ag, ag, loc.at[0]).wait()
 
 
 def grads_kernel(n_tp, local_heads,
-                 tok, n1, n2, gh, gh1, gf, act, gcat, heads, gqkv, gain, hid,
+                 h_tok, h_gain, h_hid, h_gh, h_act, h_n2, h_gcat, h_gh1, h_heads, h_n1, h_gqkv, h_gf,
                  o_hid, o_emb, o_wq, o_wk, o_wv, o_wo, o_wg, o_wu, o_wd, o_ga, o_gm,
-                 wide, tall, qbuf, kvbuf, s_wide, s_tall, s_qkv):
+                 tok, gain, hid, gains, gh, act, n2, gcat, gh1, heads, n1, gqkv, gf, wide, tall, qbuf, kvbuf, s_in, s_wide, s_tall, s_qkv, s_out):
     seq, dim = n1.shape
     rows = o_emb.shape[0]
     ffn = act.shape[1]
@@ -327,50 +404,81 @@
         if key in busy:
             busy.pop(key).wait()
 
-    tok_l = tok[...] - me * rows
+    fetch = ('act', 'gh', 'n2', 'gcat', 'tok', 'gh1', 'heads', 'gf', 'n1', 'gqkv', 'gain', 'hid')
+    pairs = ((h_act, act), (h_gh, gh), (h_n2, n2), (h_gcat, gcat), (h_tok, tok), (h_gh1, gh1), (h_heads, heads), (h_gf, gf), (h_n1, n1), (h_gqkv, gqkv),
+             (h_gain, gain), (h_hid, hid))
+    loaded = [0]
+
+    def load_to(name):
+        while loaded[0] <= fetch.index(name):
+            i = loaded[0]
+            put(('in', fetch[i]), pairs[i][0], pairs[i][1], s_in.at[i])
+            loaded[0] += 1
+
+    def use(*wanted):
+        for n in wanted:
+            load_to(n)
+        for n in wanted:
+            free(('in', n))
+
+    load_to('gcat')
     row = lax.broadcasted_iota(jnp.int32, (wr, seq), 0)
     wide_units = []
-    for u in range(act.shape[1] // wr):
-        wide_units.append((lambda u=u: dot(act[:, u * wr:(u + 1) * wr], gh[...], TN), o_wd.at[pl.ds(u * wr, wr)]))
+    for u in range(ffn // wr):
+        wide_units.append((('gh', 'act'), lambda u=u: dot(act[:, u * wr:(u + 1) * wr], gh[...], TN), o_wd.at[pl.ds(u * wr, wr)]))
     for u in range(heads.shape[1] // wr):
-        wide_units.append((lambda u=u: dot(heads[:, u * wr:(u + 1) * wr], gh1[...], TN), o_wo.at[pl.ds(u * wr, wr)]))
+        wide_units.append((('gh1', 'heads'), lambda u=u: dot(heads[:, u * wr:(u + 1) * wr], gh1[...], TN), o_wo.at[pl.ds(u * wr, wr)]))
     for u in range(rows // wr):
-        wide_units.append((lambda u=u: dot(jnp.where(row + u * wr == tok_l, 1.0, 0.0).astype(BF), gf[...]), o_emb.at[pl.ds(u * wr, wr)]))
+        wide_units.append((('gf', 'tok'), lambda u=u: dot(jnp.where(row + u * wr == tok[...] - me * rows, 1.0, 0.0).astype(BF), gf[...]),
+                           o_emb.at[pl.ds(u * wr, wr)]))
     tall_units = []
     for half, out in ((0, o_wg), (1, o_wu)):
         for u in range(dim // tr):
-            tall_units.append((lambda u=u, half=half: dot(n2[:, u * tr:(u + 1) * tr], gcat[:, half * ffn:(half + 1) * ffn], TN),
+            tall_units.append((('n2', 'gcat'), lambda u=u, half=half: dot(n2[:, u * tr:(u + 1) * tr], gcat[:, half * ffn:(half + 1) * ffn], TN),
                                out.at[pl.ds(u * tr, tr)]))
     iw = it = 0
     while iw < len(wide_units) or it < len(tall_units):
+        if iw < len(wide_units):
+            slot = iw % n_wide
+            names, fn, dst = wide_units[iw]
+            use(*names)
+            free(('w', slot))
+            with jax.named_scope(f'wide_{iw}'):
+                wide[slot] = fn()
+                put(('w', slot), wide.at[slot], dst, s_wide.at[slot])
+            iw += 1
+            if iw == 1:
+                load_to('hid')
         if it < len(tall_units):
             slot = it % n_tall
+            names, fn, dst = tall_units[it]
+            use(*names)
             free(('t', slot))
-            tall[slot] = tall_units[it][0]()
-            put(('t', slot), tall.at[slot], tall_units[it][1], s_tall.at[slot])
+            with jax.named_scope(f'tall_{it}'):
+                tall[slot] = fn()
+                put(('t', slot), tall.at[slot], dst, s_tall.at[slot])
             it += 1
-        if iw < len(wide_units):
-            slot = iw % n_wide
-            free(('w', slot))
-            wide[slot] = wide_units[iw][0]()
-            put(('w', slot), wide.at[slot], wide_units[iw][1], s_wide.at[slot])
-            iw += 1
-    qw = local_heads * hd
-    for i, out in enumerate((o_wk, o_wv)):
-        kvbuf[i] = dot(n1[...], gqkv[:, qw + i * hd:qw + (i + 1) * hd], TN)
-        put(('k', i), kvbuf.at[i], out, s_qkv.at[i])
-    for h in range(local_heads):
-        qbuf[pl.ds(h, dim, stride=local_heads), :] = dot(n1[...], gqkv[:, h * hd:(h + 1) * hd], TN)
-    put(('q', 0), qbuf, o_wq, s_qkv.at[2])
-
-    o_hid[...] = hid[...]
+    use('gain', 'hid')
     total = gain[0]
     for t in range(1, n_tp):
         total = total + gain[t]
-    o_ga[...] = total[0:1]
-    o_gm[...] = total[1:2]
-    for key in list(busy):
-        free(key)
+    gains[...] = total
+    put(('out', 0), hid, o_hid, s_out.at[0])
+    put(('out', 1), gains.at[pl.ds(0, 1)], o_ga, s_out.at[1])
+    put(('out', 2), gains.at[pl.ds(1, 1)], o_gm, s_out.at[2])
+    qw = local_heads * hd
+    use('n1', 'gqkv')
+    with jax.named_scope('qkv'):
+        for h in range(local_heads):
+            qbuf[pl.ds(h, dim, stride=local_heads), :] = dot(n1[...], gqkv[:, h * hd:(h + 1) * hd], TN)
+        put(('q', 0), qbuf, o_wq, s_qkv.at[2])
+        for i, out in enumerate((o_wk, o_wv)):
+            kvbuf[i] = dot(n1[...], gqkv[:, qw + i * hd:qw + (i + 1) * hd], TN)
+            put(('k', i), kvbuf.at[i], out, s_qkv.at[i])
+
+    with jax.named_scope('drain'):
+        for key in list(busy):
+            free(key)
 
 
 def solution(mesh):
@@ -396,7 +504,6 @@
         def sds(shape, dt=BF):
             return jax.ShapeDtypeStruct(shape, dt)
 
-        vm = pl.BlockSpec(memory_space=pltpu.VMEM)
         hb = pl.BlockSpec(memory_space=pl.ANY)
         maxc = max(RS_CHUNKS.values())
         mid = pl.pallas_call(
@@ -404,9 +511,11 @@
             name='layer',
             out_shape=[sds((n_tp, blk, dim))] * 5 + [sds((seq, ffn)), sds((seq, 2 * ffn)), sds((seq, lh * hd)), sds((seq, qkvw)),
                                                     sds((n_tp, 2, dim), F32), sds((blk, dim))],
-            in_specs=[vm] * 6 + [hb] * 8,
+            in_specs=[hb] * 14,
             out_specs=[hb] * 11,
             scratch_shapes=[
+                pltpu.VMEM((1, seq), jnp.int32), pltpu.VMEM((1, seq), jnp.int32), pltpu.VMEM((1, hd), F32),
+                pltpu.VMEM((1, dim), F32), pltpu.VMEM((1, dim), F32), pltpu.VMEM((blk, dim), BF),
                 pltpu.VMEM((rows, dim), BF), pltpu.VMEM((seq, rows), BF), pltpu.VMEM((dim * lh, hd), BF), pltpu.VMEM((dim * lh, hd), F32),
                 pltpu.VMEM((dim, qkvw), BF), pltpu.VMEM((lh * hd, dim), BF), pltpu.VMEM((dim, 2 * ffn), BF), pltpu.VMEM((ffn, dim), BF),
                 pltpu.VMEM((5, n_tp, blk, dim), BF), pltpu.VMEM((5, chips, 2, blk, dim), BF), pltpu.VMEM((5, chips, blk, dim), BF),
@@ -416,9 +525,9 @@
                 pltpu.VMEM((blk, dim), F32), pltpu.VMEM((blk, dim), F32), pltpu.VMEM((blk, dim), F32), pltpu.VMEM((blk, dim), F32),
                 pltpu.VMEM((blk, dim), F32), pltpu.VMEM((2, blk, hd), F32), pltpu.VMEM((seq, ffn), F32), pltpu.VMEM((seq, qkvw), BF),
                 pltpu.VMEM((2, seq, hd), F32), pltpu.VMEM((lh, seq, seq), F32),
-                pltpu.SemaphoreType.DMA((6, 2 * chips - 1)), pltpu.SemaphoreType.DMA((6, 2 * chips - 1)),
-                pltpu.SemaphoreType.DMA((5, maxc, chips)), pltpu.SemaphoreType.DMA((5, maxc, chips)),
-                pltpu.SemaphoreType.DMA((32,)),
+                pltpu.SemaphoreType.DMA((2, 2)), pltpu.SemaphoreType.DMA((2, 2 * chips - 1)),
+                pltpu.SemaphoreType.DMA((2, 2)), pltpu.SemaphoreType.DMA((2, maxc, chips)),
+                pltpu.SemaphoreType.DMA((24,)),
             ],
             compiler_params=pltpu.CompilerParams(collective_id=0, has_side_effects=True, vmem_limit_bytes=64 * 1024 * 1024 - 65536),
         )(tokens, positions, invf, gain_attn.reshape(1, dim), gain_mlp.reshape(1, dim), grad_hidden.reshape(blk, dim),
@@ -433,15 +542,20 @@
             out_shape=[sds((blk, dim)), sds((rows, dim), F32), sds((dim * lh, hd), F32), sds((dim, hd), F32), sds((dim, hd), F32),
                        sds((lh * hd, dim), F32), sds((dim, ffn), F32), sds((dim, ffn), F32), sds((ffn, dim), F32),
                        sds((1, dim), F32), sds((1, dim), F32)],
-            in_specs=[vm] * 12,
-            out_specs=[vm] + [hb] * 8 + [vm] * 2,
+            in_specs=[hb] * 12,
+            out_specs=[hb] * 11,
             scratch_shapes=[
+                pltpu.VMEM((1, seq), jnp.int32), pltpu.VMEM((n_tp, 2, dim), F32), pltpu.VMEM((blk, dim), BF), pltpu.VMEM((2, dim), F32),
+                pltpu.VMEM((seq, dim), BF), pltpu.VMEM((seq, ffn), BF), pltpu.VMEM((seq, dim), BF), pltpu.VMEM((seq, 2 * ffn), BF),
+                pltpu.VMEM((seq, dim), BF), pltpu.VMEM((seq, lh * hd), BF), pltpu.VMEM((seq, dim), BF), pltpu.VMEM((seq, qkvw), BF),
+                pltpu.VMEM((seq, dim), BF),
                 pltpu.VMEM((3, wide_rows, dim), F32), pltpu.VMEM((3, tall_rows, ffn), F32), pltpu.VMEM((dim * lh, hd), F32),
                 pltpu.VMEM((2, dim, hd), F32),
-                pltpu.SemaphoreType.DMA((3,)), pltpu.SemaphoreType.DMA((3,)), pltpu.SemaphoreType.DMA((3,)),
+                pltpu.SemaphoreType.DMA((12,)), pltpu.SemaphoreType.DMA((3,)), pltpu.SemaphoreType.DMA((3,)), pltpu.SemaphoreType.DMA((3,)),
+                pltpu.SemaphoreType.DMA((3,)),
             ],
             compiler_params=pltpu.CompilerParams(vmem_limit_bytes=60 * 1024 * 1024),
-        )(tokens, n1, n2, gh, gh1, gf, act, gcat, heads, gqkv, gain, hid)
+        )(tokens, gain, hid, gh, act, n2, gcat, gh1, heads, n1, gqkv, gf)
         o_hid, o_emb, o_wq, o_wk, o_wv, o_wo, o_wg, o_wu, o_wd, o_ga, o_gm = res
         return (o_hid.reshape(1, blk, dim), o_emb, o_wq.reshape(dim, lh, hd), o_wk.reshape(dim, 1, hd), o_wv.reshape(dim, 1, hd),
                 o_wo.reshape(lh, hd, dim), o_wg, o_wu, o_wd, o_ga.reshape(dim), o_gm.reshape(dim))

time: 83.4 us -> 78.6 us (0.942)
  Pallas kernels: 82.4 us -> 77.7 us
    pallas_call x1, Pallas kernels: 65.8 us -> 62.4 us  [device_fn(): pl.pallas_call(functools.partial(layer_kernel, n_tp, lh), name='layer', o...]
    pallas_call x1, Pallas kernels: 16.6 us -> 15.3 us  [device_fn(): pl.pallas_call(functools.partial(grads_kernel, n_tp, lh), name='grads', o...]
where the time goes in v2:
time: 78.6 us; the launch traced here: 78.5 us
  Pallas kernels  77.7 us (99%)
  between operations  0.82 us (1%)
    pallas_call x1, Pallas kernels, device_fn(): pl.pallas_call(functools.partial(layer_kernel, n_tp, lh), name='layer', o...  62.4 us
    pallas_call x1, Pallas kernels, device_fn(): pl.pallas_call(functools.partial(grads_kernel, n_tp, lh), name='grads', o...  15.3 us

profile of v2, /device:TPU:81, one launch (start us, length us, event | category | flops | bytes accessed | tf_op | source)
XLA Modules:
  0.0 78.5 jit_solution(16336437337917215911)
XLA Ops:
  0.6 62.4 %layer.1 = (bf16[8,16,2048]{2,1,0:T(8,128)(2,1)}, bf16[8,16,2048]{2,1,0:T(8,128)(2,1)}, bf16[8,16,2048]{2,1,0:T(8,128)(2,1)}, bf16[8,16,2048]{2,1,0:T(8,128)(2,1...) custom-call(s32[1,128]{1,0:T(1,128)} %h_tok.3, ...), custom_call_target="tpu_custom_call" | custom-call | tf_op jit(solution)/shard_map/layer/pallas_call | solution.py:509
  63.0 15.3 %grads.1 = (bf16[16,2048]{1,0:T(8,128)(2,1)}, f32[2048,2048]{1,0:T(8,128)}, f32[4096,128]{1,0:T(8,128)}, f32[2048,128]{1,0:T(8,128)}, f32[2048,128]{1,0:T(8,128)...) custom-call(s32[1,128]{1,0:T(1,128)} %h_tok.3, ...), custom_call_target="tpu_custom_call" | custom-call | tf_op jit(solution)/shard_map/grads/pallas_call | solution.py:539

commit v3 on v2

v3 whole, which is shorter than its diff:
```python
import functools

import jax
import jax.numpy as jnp
import numpy as np
from jax import lax
from jax.experimental import pallas as pl
from jax.experimental.pallas import tpu as pltpu
from jax.sharding import PartitionSpec as P

ROPE_THETA = 1000000.0
RMS_EPS = 1e-5
MESH = pl.DeviceIdType.MESH
BF = jnp.bfloat16
F32 = jnp.float32
NT = (((1,), (1,)), ((), ()))
TN = (((0,), (0,)), ((), ()))

N1, GH, N2, GH1, GF, GAIN_M, GAIN_A = range(7)
R_EMB, R_ATT, R_GN2, R_MLP, R_GN1 = range(5)
RS_CHUNKS = {R_EMB: 4, R_ATT: 2, R_GN2: 4, R_MLP: 2, R_GN1: 2}
AG_CHUNKS = {N1: 2, GH: 1, N2: 1, GH1: 2, GF: 1, GAIN_M: 1, GAIN_A: 1}


def dot(a, b, dims=(((1,), (0,)), ((), ()))):
    return lax.dot_general(a, b, dims, preferred_element_type=F32)


def scoped(name):
    def wrap(fn):
        def run(p, *rest, **kw):
            with jax.named_scope(f'{name}_{p}'):
                return fn(p, *rest, **kw)
        return run
    return wrap


def layer_kernel(n_tp, local_heads,
                 h_tok, h_pos, h_invf, h_ga, h_gm, h_gh, emb, wq4, wk, wv, wo, wg, wu, wd,
                 o_n1, o_n2, o_gh, o_gh1, o_gf, act, gcat, heads, gqkv, gain_m, gain_a, hid,
                 tok, pos, invf, ga, gm, gh_in, embv, onehot, wqr, wqf, wqkv, wov, wguv, wdv, pb, rd, sb, rr,
                 wgut, wqkvt, x0f, nrm1, nrm2, h1f, gh1f, inv, gact, qkvb, tabs, probs,
                 ag_s, ag_r, rs_s, rs_r, loc):
    chips = n_tp // 2
    seq = h_tok.shape[1]
    rows, dim = emb.shape
    ffn = wd.shape[0]
    blk = gh_in.shape[0]
    hd = wk.shape[1]
    scale = hd ** -0.5
    qw = local_heads * hd

    me = lax.axis_index('tp')
    chip = me // 2
    core = lax.rem(me, 2)
    sib = 2 * chip + 1 - core

    def peer_chip(d):
        return lax.rem(chip + d, chips)

    def peer(d):
        return 2 * peer_chip(d) + core

    order = sorted(range(1, chips), key=lambda d: -min(d, chips - d))

    barrier = pltpu.get_barrier_semaphore()
    for dev in [sib] + [peer(d) for d in range(1, chips)]:
        pl.semaphore_signal(barrier, inc=1, device_id={'tp': dev}, device_id_type=MESH)

    nloc = [1]

    def local(src, dst, slot=None):
        if slot is None:
            slot = nloc[0]
            nloc[0] += 1
        cp = pltpu.make_async_copy(src, dst, loc.at[slot])
        cp.start()
        return cp

    n_emb = RS_CHUNKS[R_EMB]
    ew = dim // n_emb

    def emb_load(j):
        return local(emb.at[:, pl.ds(j * ew, ew)], embv.at[:, pl.ds(j * ew, ew)])

    in_cp = [local(h_tok, tok)]
    emb_cp = [emb_load(0), emb_load(1)]
    in_cp += [local(a, b) for a, b in ((h_pos, pos), (h_invf, invf), (h_ga, ga), (h_gm, gm), (h_gh, gh_in))]
    in_cp[0].wait()

    tok_t = jnp.transpose(jnp.broadcast_to(tok[...].astype(F32), (seq, seq)))
    tok_t = tok_t - (me * rows).astype(F32)
    lane = lax.broadcasted_iota(jnp.int32, (seq, seq), 1).astype(F32)
    for b in range(rows // seq):
        onehot[:, b * seq:(b + 1) * seq] = jnp.where(tok_t == lane + float(b * seq), 1.0, 0.0).astype(BF)

    def remote(src, dst, s, r, dev):
        return pltpu.make_async_remote_copy(src_ref=src, dst_ref=dst, send_sem=s, recv_sem=r,
                                            device_id={'tp': dev}, device_id_type=MESH)

    def send(*args):
        remote(*args).start()

    near = sorted(range(1, chips), key=lambda d: min(d, chips - d))
    incoming = [(d, c) for d in near for c in (1, 0)]

    ag_set = {N1: 0, N2: 0, GH1: 0, GF: 0, GH: 1, GAIN_M: 1, GAIN_A: 1}
    ag = {N1: o_n1, GH: o_gh, N2: o_n2, GH1: o_gh1, GF: o_gf, GAIN_M: gain_m, GAIN_A: gain_a}
    per = 2 * chips - 1

    def ag_view(p, t, j):
        w = dim // AG_CHUNKS[p]
        return ag[p].at[t, :, pl.ds(j * w, w)]

    def ag_block(p, d, c, j):
        return ag_view(p, 2 * lax.rem(chip + chips - d, chips) + c, j)

    def ag_recv(p, j, i):
        return ag_r.at[(per * j if ag_set[p] == 0 else ag_r.shape[0] - per) + i]

    def ag_wait_sends(p):
        own, passed = ag[p].at[pl.ds(0, chips)], ag[p].at[pl.ds(0, n_tp - 2)]
        remote(own, own, ag_s.at[ag_set[p], 0], ag_recv(p, 0, 0), sib).wait_send()

        @pl.when(core == 1)
        def _():
            remote(passed, passed, ag_s.at[ag_set[p], 1], ag_recv(p, 0, 0), sib).wait_send()

    @scoped('ag_start')
    def ag_start(p):
        q = ag_set[p]
        for j in range(AG_CHUNKS[p]):
            mine = ag_view(p, me, j)
            for d in order:
                send(mine, mine, ag_s.at[q, 0], ag_recv(p, j, 2 * d - core), 2 * peer_chip(d) + 1)
            send(mine, mine, ag_s.at[q, 0], ag_recv(p, j, 0), sib)

    @scoped('ag_finish')
    def ag_finish(j, *ps, early=None, forward=True, collect=True):
        if j == 0 and forward:
            @pl.when(core == 1)
            def _():
                for k in range(AG_CHUNKS[ps[0]]):
                    for d, c in incoming:
                        for p in ps:
                            got = ag_block(p, d, c, k)
                            q = ag_set[p]
                            remote(got, got, ag_s.at[q, 1], ag_recv(p, k, 2 * d - c), sib).wait_recv()
                            send(got, got, ag_s.at[q, 1], ag_recv(p, k, 2 * d - c), sib)

        if not collect:
            return
        for p in ps:
            got = ag_view(p, sib, j)
            remote(got, got, ag_s.at[ag_set[p], 0], ag_recv(p, j, 0), sib).wait_recv()

        @pl.when(core == 0)
        def _():
            for i, (d, c) in enumerate(incoming):
                if i == 2 and early is not None:
                    early()
                for p in ps:
                    got = ag_block(p, d, c, j)
                    remote(got, got, ag_s.at[ag_set[p], 1], ag_recv(p, j, 2 * d - c), sib).wait_recv()

    def gathered(p, j=None):
        if j is None:
            return ag[p][...].reshape(seq, dim)
        w = dim // AG_CHUNKS[p]
        return ag[p][:, :, j * w:(j + 1) * w].reshape(seq, w)

    def gathered_dot(p, weight, early):
        w = dim // AG_CHUNKS[p]
        total = None
        for j in range(AG_CHUNKS[p]):
            ag_finish(j, p, early=early if j == 0 else None)
            part = weight(gathered(p, j), slice(j * w, (j + 1) * w))
            total = part if total is None else total + part
        return total

    rs_set = {R_EMB: 0, R_ATT: 0, R_GN2: 0, R_GN1: 0, R_MLP: 1}

    def rs_wait_sends(p):
        q = rs_set[p]
        remote(rd.at[p], rd.at[p], rs_s.at[q, 0], rs_r.at[q, 0, 0], sib).wait_send()
        remote(rr.at[p], rr.at[p], rs_s.at[q, 1], rs_r.at[q, 0, 0], sib).wait_send()

    def rs_cols(p, j):
        w = dim // RS_CHUNKS[p]
        return slice(j * w, (j + 1) * w)

    @scoped('rs_local')
    def rs_local(p, j, val):
        c = rs_cols(p, j)
        w = c.stop - c.start
        pb[p, :, :, :, c] = val.astype(BF).reshape(chips, 2, blk, w)
        send(pb.at[p, :, 1 - core, :, c], rd.at[p, :, :, c], rs_s.at[rs_set[p], 0], rs_r.at[rs_set[p], j, 0], sib)

    @scoped('rs_cross')
    def rs_cross(p, j):
        c = rs_cols(p, j)
        remote(rd.at[p, :, :, c], rd.at[p, :, :, c], rs_s.at[rs_set[p], 0], rs_r.at[rs_set[p], j, 0], sib).wait_recv()
        for d in order:
            to = peer_chip(d)
            both = pb[p, to, core, :, c].astype(F32) + rd[p, to, :, c].astype(F32)
            sb[p, to, :, c] = both.astype(BF)
            send(sb.at[p, to, :, c], rr.at[p, d - 1, :, c], rs_s.at[rs_set[p], 1], rs_r.at[rs_set[p], j, d], peer(d))

    @scoped('rs_finish')
    def rs_finish(p):
        parts = []
        for j in range(RS_CHUNKS[p]):
            c = rs_cols(p, j)
            total = pb[p, chip, core, :, c].astype(F32) + rd[p, chip, :, c].astype(F32)
            for d in order[::-1]:
                remote(rr.at[p, d - 1, :, c], rr.at[p, d - 1, :, c], rs_s.at[rs_set[p], 1], rs_r.at[rs_set[p], j, d], sib).wait_recv()
                total = total + rr[p, d - 1, :, c].astype(F32)
            parts.append(total)
        return jnp.concatenate(parts, axis=1)

    def rs_start(p, chunk):
        n = RS_CHUNKS[p]
        for j in range(n):
            val = chunk(rs_cols(p, j))
            if p == R_EMB and j == 0:
                with jax.named_scope('barrier'):
                    pl.semaphore_wait(barrier, chips)
            rs_local(p, j, val)
            if j > 0:
                @pl.when(core == 0)
                def _():
                    rs_cross(p, j - 1)

        @pl.when(core == 0)
        def _():
            rs_cross(p, n - 1)

        @pl.when(core == 1)
        def _():
            for j in range(n):
                rs_cross(p, j)

    def on_core(k, fn):
        @pl.when(core == k)
        def _():
            fn()

    def norm_fwd(x, gain):
        r = lax.rsqrt(jnp.mean(x * x, axis=-1, keepdims=True) + RMS_EPS)
        n = x * r
        return (n * gain).astype(BF), n, r

    def norm_bwd(g, n, r, gain):
        part = jnp.sum(g * n, axis=0, keepdims=True)
        scaled = g * gain
        return r * (scaled - n * jnp.mean(scaled * n, axis=-1, keepdims=True)), part

    w_cp = {}

    def emb_chunk(c):
        j = c.start // ew
        emb_cp[j].wait()
        if j + 2 < n_emb:
            emb_cp.append(emb_load(j + 2))
        if j == n_emb - 2:
            w_cp['g'] = local(wg, wguv.at[:, pl.ds(0, ffn)])
            w_cp['u'] = local(wu, wguv.at[:, pl.ds(ffn, ffn)])
        if j == n_emb - 1:
            w_cp['k'] = local(wk, wqkv.at[:, pl.ds(qw, hd)])
            w_cp['v'] = local(wv, wqkv.at[:, pl.ds(qw + hd, hd)])
            w_cp['q'] = local(wq4, wqr)
            w_cp['o'] = local(wo, wov)
            w_cp['d'] = local(wd, wdv)
        return dot(onehot[...], embv[:, c])

    rs_start(R_EMB, emb_chunk)

    tw = 256
    eye = (lax.broadcasted_iota(jnp.int32, (tw, tw), 0) == lax.broadcasted_iota(jnp.int32, (tw, tw), 1)).astype(F32).astype(BF)
    w_cp['g'].wait()
    w_cp['u'].wait()
    with jax.named_scope('wgut'):
        for b in range(2 * ffn // tw):
            wgut[b * tw:(b + 1) * tw, :] = dot(eye, wguv[:, b * tw:(b + 1) * tw], NT).astype(BF)

    for cp in in_cp[3:]:
        cp.wait()
    x0 = rs_finish(R_EMB)
    x0f[...] = x0
    n1b, n1, r1 = norm_fwd(x0, ga[...])
    o_n1[me] = n1b
    nrm1[...] = n1
    inv[0] = jnp.broadcast_to(r1, (blk, hd))
    ag_start(N1)
    o_gh[me] = gh_in[...]
    w_cp['k'].wait()
    w_cp['v'].wait()
    in_cp[1].wait()
    in_cp[2].wait()
    pos_t = jnp.transpose(jnp.broadcast_to(pos[...].astype(F32), (seq, seq)))
    angle = pos_t * invf[...]
    half = lax.broadcasted_iota(jnp.int32, (seq, hd), 1) < hd // 2
    tabs[0] = jnp.cos(angle)
    sin = jnp.sin(angle)
    tabs[1] = jnp.where(half, -sin, sin)
    w_cp['q'].wait()
    wqf[...] = wqr[...].astype(F32)
    for h in range(local_heads):
        wqkv[:, h * hd:(h + 1) * hd] = wqf[pl.ds(h, dim, stride=local_heads), :].astype(BF)


    with jax.named_scope('wqkvt'):
        for b in range((qw + 2 * hd) // tw):
            wqkvt[b * tw:(b + 1) * tw, :] = dot(eye, wqkv[:, b * tw:(b + 1) * tw], NT).astype(BF)

    def rotate(v, sign):
        return v * tabs[0] + sign * (pltpu.roll(v, hd // 2, 1) * tabs[1])

    qkv = gathered_dot(N1, lambda a, k: dot(a, wqkv[k, :]), lambda: ag_start(GH))
    on_core(1, lambda: ag_start(GH))
    for h in range(local_heads + 1):
        qkvb[:, h * hd:(h + 1) * hd] = rotate(qkv[:, h * hd:(h + 1) * hd], 1.0).astype(BF)
    qkvb[:, qw + hd:] = qkv[:, qw + hd:].astype(BF)
    kb = qkvb[:, qw:qw + hd]
    vb = qkvb[:, qw + hd:]
    causal = lax.broadcasted_iota(jnp.int32, (seq, seq), 0) >= lax.broadcasted_iota(jnp.int32, (seq, seq), 1)
    for h in range(local_heads):
        s = dot(qkvb[:, h * hd:(h + 1) * hd], kb, NT) * scale
        s = jnp.where(causal, s, -1e30)
        e = jnp.exp(s - jnp.max(s, axis=-1, keepdims=True))
        pr = e / jnp.sum(e, axis=-1, keepdims=True)
        probs[h] = pr
        heads[:, h * hd:(h + 1) * hd] = dot(pr.astype(BF), vb).astype(BF)
    w_cp['o'].wait()
    rs_wait_sends(R_EMB)
    rs_start(R_ATT, lambda c: dot(heads[...], wov[:, c]))

    ag_finish(0, GH)
    w_cp['d'].wait()

    h1 = (x0f[...] + rs_finish(R_ATT).astype(BF).astype(F32)).astype(BF).astype(F32)
    h1f[...] = h1
    n2b, n2, r2 = norm_fwd(h1, gm[...])
    o_n2[me] = n2b
    nrm2[...] = n2
    inv[1] = jnp.broadcast_to(r2, (blk, hd))
    ag_wait_sends(N1)
    ag_start(N2)
    with jax.named_scope('gact'):
        gact[...] = dot(gathered(GH), wdv[...], NT).astype(BF).astype(F32)

    ag_finish(0, N2)
    fw = 256
    for j in range(ffn // fw):
        c = slice(j * fw, (j + 1) * fw)
        cu = slice(ffn + j * fw, ffn + (j + 1) * fw)
        gate = dot(gathered(N2), wguv[:, c])
        up = dot(gathered(N2), wguv[:, cu])
        sig = jax.nn.sigmoid(gate)
        ga_act = gate * sig
        act[:, c] = (ga_act * up).astype(BF)
        g = gact[:, c]
        gcat[:, cu] = (g * ga_act).astype(BF)
        gcat[:, c] = (g * up * sig * (1.0 + gate * (1.0 - sig))).astype(BF)
    rs_wait_sends(R_ATT)
    rs_start(R_GN2, lambda c: dot(gcat[...], wgut[:, c]))
    for j in range(RS_CHUNKS[R_MLP]):
        rs_local(R_MLP, j, dot(act[...], wdv[:, rs_cols(R_MLP, j)]))

    gn2 = rs_finish(R_GN2).astype(BF).astype(F32)
    g_in, gain_part = norm_bwd(gn2, nrm2[...], inv[1][:, :1], gm[...])
    gain_m[me] = gain_part
    gh1 = (gh_in[...].astype(F32) + g_in).astype(BF)
    gh1f[...] = gh1.astype(F32)
    o_gh1[me] = gh1
    ag_wait_sends(N2)
    ag_start(GH1)
    ag_wait_sends(GH)
    ag_start(GAIN_M)
    def mlp_cross():
        for j in range(RS_CHUNKS[R_MLP]):
            rs_cross(R_MLP, j)

    ghd = gathered_dot(GH1, lambda a, k: dot(a, wov[:, k], NT), mlp_cross).astype(BF)
    on_core(1, mlp_cross)
    ag_finish(0, GAIN_M, collect=False)

    gv = jnp.zeros((seq, hd), F32)
    gk = jnp.zeros((seq, hd), F32)
    for h in range(local_heads):
        g = ghd[:, h * hd:(h + 1) * hd]
        pr = probs[h]
        gp = dot(g, vb, NT).astype(BF).astype(F32)
        gv = gv + dot(pr.astype(BF), g, TN)
        gs = (pr * (gp - jnp.sum(gp * pr, axis=-1, keepdims=True)) * scale).astype(BF)
        gq = dot(gs, kb).astype(BF).astype(F32)
        gk = gk + dot(gs, qkvb[:, h * hd:(h + 1) * hd], TN)
        gqkv[:, h * hd:(h + 1) * hd] = rotate(gq, -1.0).astype(BF)
    gqkv[:, qw:qw + hd] = rotate(gk.astype(BF).astype(F32), -1.0).astype(BF)
    gqkv[:, qw + hd:] = gv.astype(BF)
    ag_finish(0, GAIN_M, forward=False)
    rs_wait_sends(R_GN2)
    rs_start(R_GN1, lambda c: dot(gqkv[...], wqkvt[:, c]))
    hid[...] = (h1f[...] + rs_finish(R_MLP).astype(BF).astype(F32)).astype(BF)

    gn1 = rs_finish(R_GN1).astype(BF).astype(F32)
    g_in, gain_part = norm_bwd(gn1, nrm1[...], inv[0][:, :1], ga[...])
    gain_a[me] = gain_part
    o_gf[me] = (gh1f[...] + g_in).astype(BF)
    ag_wait_sends(GAIN_M)
    ag_wait_sends(GH1)
    ag_start(GAIN_A)
    ag_start(GF)
    ag_finish(0, GAIN_A, GF)
    with jax.named_scope('tail_send'):
        rs_wait_sends(R_GN1)
        rs_wait_sends(R_MLP)
        ag_wait_sends(GAIN_A)
        ag_wait_sends(GF)


def grads_kernel(n_tp, local_heads,
                 tok, gain_m, gain_a, hid, gh, act, n2, gcat, gh1, heads, n1, gqkv, gf,
                 o_hid, o_emb, o_wq, o_wk, o_wv, o_wo, o_wg, o_wu, o_wd, o_ga, o_gm,
                 gains, wide, tall, qbuf, kvbuf, s_wide, s_tall, s_qkv, s_out):
    seq, dim = n1.shape
    rows = o_emb.shape[0]
    ffn = act.shape[1]
    hd = gqkv.shape[1] // (local_heads + 2)
    me = lax.axis_index('tp')
    n_wide, wr = wide.shape[0], wide.shape[1]
    n_tall, tr = tall.shape[0], tall.shape[1]
    busy = {}

    def put(key, src, dst, sem):
        cp = pltpu.make_async_copy(src, dst, sem)
        cp.start()
        busy[key] = cp

    def free(key):
        if key in busy:
            busy.pop(key).wait()

    row = lax.broadcasted_iota(jnp.int32, (wr, seq), 0)
    wide_units = []
    for u in range(ffn // wr):
        wide_units.append((lambda u=u: dot(act[:, u * wr:(u + 1) * wr], gh[...], TN), o_wd.at[pl.ds(u * wr, wr)]))
    for u in range(heads.shape[1] // wr):
        wide_units.append((lambda u=u: dot(heads[:, u * wr:(u + 1) * wr], gh1[...], TN), o_wo.at[pl.ds(u * wr, wr)]))
    for u in range(rows // wr):
        wide_units.append((lambda u=u: dot(jnp.where(row + u * wr == tok[...] - me * rows, 1.0, 0.0).astype(BF), gf[...]),
                           o_emb.at[pl.ds(u * wr, wr)]))
    tall_units = []
    for half, out in ((0, o_wg), (1, o_wu)):
        for u in range(dim // tr):
            tall_units.append((lambda u=u, half=half: dot(n2[:, u * tr:(u + 1) * tr], gcat[:, half * ffn:(half + 1) * ffn], TN),
                               out.at[pl.ds(u * tr, tr)]))
    iw = it = 0
    while iw < len(wide_units) or it < len(tall_units):
        if iw < len(wide_units):
            slot = iw % n_wide
            fn, dst = wide_units[iw]
            free(('w', slot))
            with jax.named_scope(f'wide_{iw}'):
                wide[slot] = fn()
                put(('w', slot), wide.at[slot], dst, s_wide.at[slot])
            iw += 1
        if it < len(tall_units):
            slot = it % n_tall
            fn, dst = tall_units[it]
            free(('t', slot))
            with jax.named_scope(f'tall_{it}'):
                tall[slot] = fn()
                put(('t', slot), tall.at[slot], dst, s_tall.at[slot])
            it += 1
    for i, part in enumerate((gain_a, gain_m)):
        total = part[0]
        for t in range(1, n_tp):
            total = total + part[t]
        gains[i:i + 1, :] = total
    put(('out', 0), hid, o_hid, s_out.at[0])
    put(('out', 1), gains.at[pl.ds(0, 1)], o_ga, s_out.at[1])
    put(('out', 2), gains.at[pl.ds(1, 1)], o_gm, s_out.at[2])
    qw = local_heads * hd
    with jax.named_scope('qkv'):
        for h in range(local_heads):
            qbuf[pl.ds(h, dim, stride=local_heads), :] = dot(n1[...], gqkv[:, h * hd:(h + 1) * hd], TN)
        put(('q', 0), qbuf, o_wq, s_qkv.at[2])
        for i, out in enumerate((o_wk, o_wv)):
            kvbuf[i] = dot(n1[...], gqkv[:, qw + i * hd:qw + (i + 1) * hd], TN)
            put(('k', i), kvbuf.at[i], out, s_qkv.at[i])

    with jax.named_scope('drain'):
        for key in list(busy):
            free(key)


def solution(mesh):
    n_tp = mesh.shape['tp']
    chips = n_tp // 2
    in_specs = (P('dp', None), P('dp', None), P('tp', None), P(None), P(None),
                P(None, 'tp', None), P(None, 'tp', None), P(None, 'tp', None), P('tp', None, None),
                P(None, 'tp'), P(None, 'tp'), P('tp', None), P('dp', 'tp', None))
    out_specs = (P('dp', 'tp', None), P(('dp', 'tp'), None),
                 P('dp', 'tp', None), P('dp', 'tp', None), P('dp', 'tp', None), P(('dp', 'tp'), None, None),
                 P('dp', 'tp'), P('dp', 'tp'), P(('dp', 'tp'), None), P('dp'), P('dp'))

    def device_fn(tokens, positions, emb, gain_attn, gain_mlp, w_query, w_key, w_value, w_out, w_gate, w_up, w_down, grad_hidden):
        seq = tokens.shape[1]
        rows, dim = emb.shape
        lh, hd = w_query.shape[1], w_query.shape[2]
        ffn = w_down.shape[0]
        blk = grad_hidden.shape[1]
        qkvw = (lh + 2) * hd
        inv_freq = (np.float32(ROPE_THETA) ** (-np.arange(hd // 2, dtype=np.float32) * np.float32(2.0 / hd))).astype(np.float32)
        invf = jnp.asarray(np.concatenate([inv_freq, inv_freq])[None, :])

        def sds(shape, dt=BF):
            return jax.ShapeDtypeStruct(shape, dt)

        hb = pl.BlockSpec(memory_space=pltpu.HBM)
        vm = pl.BlockSpec(memory_space=pltpu.VMEM)
        maxc = max(RS_CHUNKS.values())
        mid = pl.pallas_call(
            functools.partial(layer_kernel, n_tp, lh),
            name='layer',
            out_shape=[sds((n_tp, blk, dim))] * 5 + [sds((seq, ffn)), sds((seq, 2 * ffn)), sds((seq, lh * hd)), sds((seq, qkvw)),
                                                    sds((n_tp, 1, dim), F32), sds((n_tp, 1, dim), F32), sds((blk, dim))],
            in_specs=[hb] * 14,
            out_specs=[vm] * 12,
            scratch_shapes=[
                pltpu.VMEM((1, seq), jnp.int32), pltpu.VMEM((1, seq), jnp.int32), pltpu.VMEM((1, hd), F32),
                pltpu.VMEM((1, dim), F32), pltpu.VMEM((1, dim), F32), pltpu.VMEM((blk, dim), BF),
                pltpu.VMEM((rows, dim), BF), pltpu.VMEM((seq, rows), BF), pltpu.VMEM((dim * lh, hd), BF), pltpu.VMEM((dim * lh, hd), F32),
                pltpu.VMEM((dim, qkvw), BF), pltpu.VMEM((lh * hd, dim), BF), pltpu.VMEM((dim, 2 * ffn), BF), pltpu.VMEM((ffn, dim), BF),
                pltpu.VMEM((5, chips, 2, blk, dim), BF), pltpu.VMEM((5, chips, blk, dim), BF),
                pltpu.VMEM((5, chips, blk, dim), BF), pltpu.VMEM((5, chips - 1, blk, dim), BF),
                pltpu.VMEM((2 * ffn, dim), BF), pltpu.VMEM((qkvw, dim), BF), pltpu.VMEM((blk, dim), F32), pltpu.VMEM((blk, dim), F32), pltpu.VMEM((blk, dim), F32), pltpu.VMEM((blk, dim), F32),
                pltpu.VMEM((blk, dim), F32), pltpu.VMEM((2, blk, hd), F32), pltpu.VMEM((seq, ffn), F32), pltpu.VMEM((seq, qkvw), BF),
                pltpu.VMEM((2, seq, hd), F32), pltpu.VMEM((lh, seq, seq), F32),
                pltpu.SemaphoreType.DMA((2, 2)), pltpu.SemaphoreType.DMA(((max(AG_CHUNKS.values()) + 1) * (2 * chips - 1),)),
                pltpu.SemaphoreType.DMA((2, 2)), pltpu.SemaphoreType.DMA((2, maxc, chips)),
                pltpu.SemaphoreType.DMA((18,)),
            ],
            compiler_params=pltpu.CompilerParams(collective_id=0, has_side_effects=True, vmem_limit_bytes=44 * 1024 * 1024),
        )(*(pltpu.with_memory_space_constraint(a, pltpu.HBM) for a in (
            tokens, positions, invf, gain_attn.reshape(1, dim), gain_mlp.reshape(1, dim), grad_hidden.reshape(blk, dim),
            emb, w_query.reshape(dim * lh, hd), w_key.reshape(dim, hd), w_value.reshape(dim, hd), w_out.reshape(lh * hd, dim),
            w_gate, w_up, w_down)))
        n1, n2, gh, gh1, gf, act, gcat, heads, gqkv, gain_m, gain_a, hid = mid
        n1, n2, gh, gh1, gf = (a.reshape(seq, dim) for a in (n1, n2, gh, gh1, gf))
        wide_rows, tall_rows = 256, 512
        res = pl.pallas_call(
            functools.partial(grads_kernel, n_tp, lh),
            name='grads',
            out_shape=[sds((blk, dim)), sds((rows, dim), F32), sds((dim * lh, hd), F32), sds((dim, hd), F32), sds((dim, hd), F32),
                       sds((lh * hd, dim), F32), sds((dim, ffn), F32), sds((dim, ffn), F32), sds((ffn, dim), F32),
                       sds((1, dim), F32), sds((1, dim), F32)],
            in_specs=[vm] * 13,
            out_specs=[hb] * 11,
            scratch_shapes=[
                pltpu.VMEM((2, dim), F32),
                pltpu.VMEM((3, wide_rows, dim), F32), pltpu.VMEM((3, tall_rows, ffn), F32), pltpu.VMEM((dim * lh, hd), F32),
                pltpu.VMEM((2, dim, hd), F32),
                pltpu.SemaphoreType.DMA((3,)), pltpu.SemaphoreType.DMA((3,)), pltpu.SemaphoreType.DMA((3,)),
                pltpu.SemaphoreType.DMA((3,)),
            ],
            compiler_params=pltpu.CompilerParams(vmem_limit_bytes=24 * 1024 * 1024),
        )(tokens, gain_m, gain_a, hid, gh, act, n2, gcat, gh1, heads, n1, gqkv, gf)
        o_hid, o_emb, o_wq, o_wk, o_wv, o_wo, o_wg, o_wu, o_wd, o_ga, o_gm = res
        return (o_hid.reshape(1, blk, dim), o_emb, o_wq.reshape(dim, lh, hd), o_wk.reshape(dim, 1, hd), o_wv.reshape(dim, 1, hd),
                o_wo.reshape(lh, hd, dim), o_wg, o_wu, o_wd, o_ga.reshape(dim), o_gm.reshape(dim))

    return jax.shard_map(device_fn, mesh=mesh, in_specs=in_specs, out_specs=out_specs, check_vma=False)
```

time: 78.6 us -> 76.3 us (0.971)
  Pallas kernels: 77.7 us -> 75.4 us
    pallas_call x1, Pallas kernels: 15.3 us -> 14 us  [device_fn(): pl.pallas_call(functools.partial(grads_kernel, n_tp, lh), name='grads', o...]
    pallas_call x1, Pallas kernels: 62.4 us -> 61.4 us  [device_fn(): pl.pallas_call(functools.partial(layer_kernel, n_tp, lh), name='layer', o...]
where the time goes in v3:
time: 76.3 us; the launch traced here: 76.2 us
  Pallas kernels  75.4 us (99%)
  between operations  0.83 us (1%)
    pallas_call x1, Pallas kernels, device_fn(): pl.pallas_call(functools.partial(layer_kernel, n_tp, lh), name='layer', o...  61.4 us
    pallas_call x1, Pallas kernels, device_fn(): pl.pallas_call(functools.partial(grads_kernel, n_tp, lh), name='grads', o...  14 us

profile of v3, /device:TPU:81, one launch (start us, length us, event | category | flops | bytes accessed | tf_op | source)
XLA Modules:
  0.0 76.2 jit_solution(2748031713561485897)
XLA Ops:
  0.6 0.0 copy-start
  0.7 61.4 %layer.1 = (bf16[8,16,2048]{2,1,0:T(8,128)(2,1)S(1)}, bf16[8,16,2048]{2,1,0:T(8,128)(2,1)S(1)}, bf16[8,16,2048]{2,1,0:T(8,128)(2,1)S(1)}, bf16[8,16,2048]{2,1,0:...) custom-call(s32[1,128]{1,0:T(1,128)} %tok.1, ...), custom_call_target="tpu_custom_call" | custom-call | tf_op jit(solution)/shard_map/layer/pallas_call | solution.py:524
  62.0 0.0 copy-done
  62.0 14.0 %grads.1 = (bf16[16,2048]{1,0:T(8,128)(2,1)}, f32[2048,2048]{1,0:T(8,128)}, f32[4096,128]{1,0:T(8,128)}, f32[2048,128]{1,0:T(8,128)}, f32[2048,128]{1,0:T(8,128)...) custom-call(s32[1,128]{1,0:T(1,128)S(1)} %copy-done, ...), custom_call_target="tpu_custom_call" | custom-call | tf_op jit(solution)/shard_map/grads/pallas_call | solution.py:553
Async XLA Ops:
  0.6 61.4 %copy-start = (s32[1,128]{1,0:T(1,128)S(1)}, s32[1,128]{1,0:T(1,128)}, u32[]{:S(2)}) copy-start(s32[1,128]{1,0:T(1,128)} %tok.1) | copy-start | bytes 1540

commit v4 on v3

--- a/solution.py
+++ b/solution.py
@@ -19,7 +19,7 @@
 N1, GH, N2, GH1, GF, GAIN_M, GAIN_A = range(7)
 R_EMB, R_ATT, R_GN2, R_MLP, R_GN1 = range(5)
 RS_CHUNKS = {R_EMB: 4, R_ATT: 2, R_GN2: 4, R_MLP: 2, R_GN1: 2}
-AG_CHUNKS = {N1: 2, GH: 1, N2: 1, GH1: 2, GF: 1, GAIN_M: 1, GAIN_A: 1}
+AG_CHUNKS = {N1: 4, GH: 1, N2: 1, GH1: 2, GF: 1, GAIN_M: 1, GAIN_A: 1}
 
 
 def dot(a, b, dims=(((1,), (0,)), ((), ()))):
@@ -39,7 +39,7 @@
                  h_tok, h_pos, h_invf, h_ga, h_gm, h_gh, emb, wq4, wk, wv, wo, wg, wu, wd,
                  o_n1, o_n2, o_gh, o_gh1, o_gf, act, gcat, heads, gqkv, gain_m, gain_a, hid,
                  tok, pos, invf, ga, gm, gh_in, embv, onehot, wqr, wqf, wqkv, wov, wguv, wdv, pb, rd, sb, rr,
-                 wgut, wqkvt, x0f, nrm1, nrm2, h1f, gh1f, inv, gact, qkvb, tabs, probs,
+                 x0g, wgut, wqkvt, x0f, nrm1, nrm2, h1f, gh1f, inv, gact, qkvb, tabs, probs,
                  ag_s, ag_r, rs_s, rs_r, loc):
     chips = n_tp // 2
     seq = h_tok.shape[1]
@@ -84,7 +84,7 @@
         return local(emb.at[:, pl.ds(j * ew, ew)], embv.at[:, pl.ds(j * ew, ew)])
 
     in_cp = [local(h_tok, tok)]
-    emb_cp = [emb_load(0), emb_load(1)]
+    emb_cp = [emb_load(j) for j in range(3)]
     in_cp += [local(a, b) for a, b in ((h_pos, pos), (h_invf, invf), (h_ga, ga), (h_gm, gm), (h_gh, gh_in))]
     in_cp[0].wait()
 
@@ -105,7 +105,7 @@
     incoming = [(d, c) for d in near for c in (1, 0)]
 
     ag_set = {N1: 0, N2: 0, GH1: 0, GF: 0, GH: 1, GAIN_M: 1, GAIN_A: 1}
-    ag = {N1: o_n1, GH: o_gh, N2: o_n2, GH1: o_gh1, GF: o_gf, GAIN_M: gain_m, GAIN_A: gain_a}
+    ag = {N1: x0g, GH: o_gh, N2: o_n2, GH1: o_gh1, GF: o_gf, GAIN_M: gain_m, GAIN_A: gain_a}
     per = 2 * chips - 1
 
     def ag_view(p, t, j):
@@ -127,9 +127,9 @@
             remote(passed, passed, ag_s.at[ag_set[p], 1], ag_recv(p, 0, 0), sib).wait_send()
 
     @scoped('ag_start')
-    def ag_start(p):
+    def ag_start(p, only=None):
         q = ag_set[p]
-        for j in range(AG_CHUNKS[p]):
+        for j in range(AG_CHUNKS[p]) if only is None else (only,):
             mine = ag_view(p, me, j)
             for d in order:
                 send(mine, mine, ag_s.at[q, 0], ag_recv(p, j, 2 * d - core), 2 * peer_chip(d) + 1)
@@ -207,9 +207,9 @@
             send(sb.at[p, to, :, c], rr.at[p, d - 1, :, c], rs_s.at[rs_set[p], 1], rs_r.at[rs_set[p], j, d], peer(d))
 
     @scoped('rs_finish')
-    def rs_finish(p):
+    def rs_finish(p, only=None):
         parts = []
-        for j in range(RS_CHUNKS[p]):
+        for j in range(RS_CHUNKS[p]) if only is None else (only,):
             c = rs_cols(p, j)
             total = pb[p, chip, core, :, c].astype(F32) + rd[p, chip, :, c].astype(F32)
             for d in order[::-1]:
@@ -260,41 +260,21 @@
     def emb_chunk(c):
         j = c.start // ew
         emb_cp[j].wait()
-        if j + 2 < n_emb:
-            emb_cp.append(emb_load(j + 2))
+        if j + 3 < n_emb:
+            emb_cp.append(emb_load(j + 3))
         if j == n_emb - 2:
-            w_cp['g'] = local(wg, wguv.at[:, pl.ds(0, ffn)])
-            w_cp['u'] = local(wu, wguv.at[:, pl.ds(ffn, ffn)])
-        if j == n_emb - 1:
             w_cp['k'] = local(wk, wqkv.at[:, pl.ds(qw, hd)])
             w_cp['v'] = local(wv, wqkv.at[:, pl.ds(qw + hd, hd)])
             w_cp['q'] = local(wq4, wqr)
+        if j == n_emb - 1:
             w_cp['o'] = local(wo, wov)
+            w_cp['g'] = local(wg, wguv.at[:, pl.ds(0, ffn)])
+            w_cp['u'] = local(wu, wguv.at[:, pl.ds(ffn, ffn)])
             w_cp['d'] = local(wd, wdv)
         return dot(onehot[...], embv[:, c])
 
     rs_start(R_EMB, emb_chunk)
 
-    tw = 256
-    eye = (lax.broadcasted_iota(jnp.int32, (tw, tw), 0) == lax.broadcasted_iota(jnp.int32, (tw, tw), 1)).astype(F32).astype(BF)
-    w_cp['g'].wait()
-    w_cp['u'].wait()
-    with jax.named_scope('wgut'):
-        for b in range(2 * ffn // tw):
-            wgut[b * tw:(b + 1) * tw, :] = dot(eye, wguv[:, b * tw:(b + 1) * tw], NT).astype(BF)
-
-    for cp in in_cp[3:]:
-        cp.wait()
-    x0 = rs_finish(R_EMB)
-    x0f[...] = x0
-    n1b, n1, r1 = norm_fwd(x0, ga[...])
-    o_n1[me] = n1b
-    nrm1[...] = n1
-    inv[0] = jnp.broadcast_to(r1, (blk, hd))
-    ag_start(N1)
-    o_gh[me] = gh_in[...]
-    w_cp['k'].wait()
-    w_cp['v'].wait()
     in_cp[1].wait()
     in_cp[2].wait()
     pos_t = jnp.transpose(jnp.broadcast_to(pos[...].astype(F32), (seq, seq)))
@@ -303,12 +283,28 @@
     tabs[0] = jnp.cos(angle)
     sin = jnp.sin(angle)
     tabs[1] = jnp.where(half, -sin, sin)
+    for cp in in_cp[3:]:
+        cp.wait()
+    for j in range(RS_CHUNKS[R_EMB]):
+        part = rs_finish(R_EMB, j)
+        x0f[:, rs_cols(R_EMB, j)] = part
+        x0g[me, :, rs_cols(R_EMB, j)] = part.astype(BF)
+        ag_start(N1, j)
+    x0 = x0f[...]
+    n1b, n1, r1 = norm_fwd(x0, ga[...])
+    nrm1[...] = n1
+    inv[0] = jnp.broadcast_to(r1, (blk, hd))
+    o_gh[me] = gh_in[...]
+    w_cp['k'].wait()
+    w_cp['v'].wait()
     w_cp['q'].wait()
     wqf[...] = wqr[...].astype(F32)
     for h in range(local_heads):
         wqkv[:, h * hd:(h + 1) * hd] = wqf[pl.ds(h, dim, stride=local_heads), :].astype(BF)
 
 
+    tw = 256
+    eye = (lax.broadcasted_iota(jnp.int32, (tw, tw), 0) == lax.broadcasted_iota(jnp.int32, (tw, tw), 1)).astype(F32).astype(BF)
     with jax.named_scope('wqkvt'):
         for b in range((qw + 2 * hd) // tw):
             wqkvt[b * tw:(b + 1) * tw, :] = dot(eye, wqkv[:, b * tw:(b + 1) * tw], NT).astype(BF)
@@ -316,7 +312,18 @@
     def rotate(v, sign):
         return v * tabs[0] + sign * (pltpu.roll(v, hd // 2, 1) * tabs[1])
 
-    qkv = gathered_dot(N1, lambda a, k: dot(a, wqkv[k, :]), lambda: ag_start(GH))
+    square = None
+    for j in range(AG_CHUNKS[N1]):
+        ag_finish(j, N1, early=(lambda: ag_start(GH)) if j == 0 else None)
+        part = gathered(N1, j).astype(F32)
+        part = jnp.sum(part * part, axis=-1, keepdims=True)
+        square = part if square is None else square + part
+    rms = lax.rsqrt(square * (1.0 / dim) + RMS_EPS)
+    cw = dim // AG_CHUNKS[N1]
+    for j in range(AG_CHUNKS[N1]):
+        c = slice(j * cw, (j + 1) * cw)
+        o_n1[:, :, c] = (gathered(N1, j).astype(F32) * rms * ga[:, c]).astype(BF).reshape(n_tp, blk, cw)
+    qkv = dot(o_n1[...].reshape(seq, dim), wqkv[...])
     on_core(1, lambda: ag_start(GH))
     for h in range(local_heads + 1):
         qkvb[:, h * hd:(h + 1) * hd] = rotate(qkv[:, h * hd:(h + 1) * hd], 1.0).astype(BF)
@@ -335,6 +342,11 @@
     rs_wait_sends(R_EMB)
     rs_start(R_ATT, lambda c: dot(heads[...], wov[:, c]))
 
+    w_cp['g'].wait()
+    w_cp['u'].wait()
+    with jax.named_scope('wgut'):
+        for b in range(2 * ffn // tw):
+            wgut[b * tw:(b + 1) * tw, :] = dot(eye, wguv[:, b * tw:(b + 1) * tw], NT).astype(BF)
     ag_finish(0, GH)
     w_cp['d'].wait()
 
@@ -535,7 +547,7 @@
                 pltpu.VMEM((dim, qkvw), BF), pltpu.VMEM((lh * hd, dim), BF), pltpu.VMEM((dim, 2 * ffn), BF), pltpu.VMEM((ffn, dim), BF),
                 pltpu.VMEM((5, chips, 2, blk, dim), BF), pltpu.VMEM((5, chips, blk, dim), BF),
                 pltpu.VMEM((5, chips, blk, dim), BF), pltpu.VMEM((5, chips - 1, blk, dim), BF),
-                pltpu.VMEM((2 * ffn, dim), BF), pltpu.VMEM((qkvw, dim), BF), pltpu.VMEM((blk, dim), F32), pltpu.VMEM((blk, dim), F32), pltpu.VMEM((blk, dim), F32), pltpu.VMEM((blk, dim), F32),
+                pltpu.VMEM((n_tp, blk, dim), BF), pltpu.VMEM((2 * ffn, dim), BF), pltpu.VMEM((qkvw, dim), BF), pltpu.VMEM((blk, dim), F32), pltpu.VMEM((blk, dim), F32), pltpu.VMEM((blk, dim), F32), pltpu.VMEM((blk, dim), F32),
                 pltpu.VMEM((blk, dim), F32), pltpu.VMEM((2, blk, hd), F32), pltpu.VMEM((seq, ffn), F32), pltpu.VMEM((seq, qkvw), BF),
                 pltpu.VMEM((2, seq, hd), F32), pltpu.VMEM((lh, seq, seq), F32),
                 pltpu.SemaphoreType.DMA((2, 2)), pltpu.SemaphoreType.DMA(((max(AG_CHUNKS.values()) + 1) * (2 * chips - 1),)),

time: 76.3 us -> 74.3 us (0.974)
  Pallas kernels: 75.4 us -> 73.4 us
    pallas_call x1, Pallas kernels: 61.4 us -> 59.4 us  [device_fn(): pl.pallas_call(functools.partial(layer_kernel, n_tp, lh), name='layer', o...]
where the time goes in v4:
time: 74.3 us; the launch traced here: 74.2 us
  Pallas kernels  73.4 us (99%)
  between operations  0.83 us (1%)
    pallas_call x1, Pallas kernels, device_fn(): pl.pallas_call(functools.partial(layer_kernel, n_tp, lh), name='layer', o...  59.4 us
    pallas_call x1, Pallas kernels, device_fn(): pl.pallas_call(functools.partial(grads_kernel, n_tp, lh), name='grads', o...  14 us

profile of v4, /device:TPU:81, one launch (start us, length us, event | category | flops | bytes accessed | tf_op | source)
XLA Modules:
  0.0 74.2 jit_solution(14704596384854512126)
XLA Ops:
  0.6 0.0 copy-start
  0.7 59.4 %layer.1 = (bf16[8,16,2048]{2,1,0:T(8,128)(2,1)S(1)}, bf16[8,16,2048]{2,1,0:T(8,128)(2,1)S(1)}, bf16[8,16,2048]{2,1,0:T(8,128)(2,1)S(1)}, bf16[8,16,2048]{2,1,0:...) custom-call(s32[1,128]{1,0:T(1,128)} %tok.1, ...), custom_call_target="tpu_custom_call" | custom-call | tf_op jit(solution)/shard_map/layer/pallas_call | solution.py:536
  60.0 0.0 copy-done
  60.0 14.0 %grads.1 = (bf16[16,2048]{1,0:T(8,128)(2,1)}, f32[2048,2048]{1,0:T(8,128)}, f32[4096,128]{1,0:T(8,128)}, f32[2048,128]{1,0:T(8,128)}, f32[2048,128]{1,0:T(8,128)...) custom-call(s32[1,128]{1,0:T(1,128)S(1)} %copy-done, ...), custom_call_target="tpu_custom_call" | custom-call | tf_op jit(solution)/shard_map/grads/pallas_call | solution.py:565
Async XLA Ops:
  0.6 59.4 %copy-start = (s32[1,128]{1,0:T(1,128)S(1)}, s32[1,128]{1,0:T(1,128)}, u32[]{:S(2)}) copy-start(s32[1,128]{1,0:T(1,128)} %tok.1) | copy-start | bytes 1540

commit v5 on v4

--- a/solution.py
+++ b/solution.py
@@ -16,10 +16,10 @@
 NT = (((1,), (1,)), ((), ()))
 TN = (((0,), (0,)), ((), ()))
 
-N1, GH, N2, GH1, GF, GAIN_M, GAIN_A = range(7)
+N1, GH, N2, GH1, GF = range(5)
 R_EMB, R_ATT, R_GN2, R_MLP, R_GN1 = range(5)
-RS_CHUNKS = {R_EMB: 4, R_ATT: 2, R_GN2: 4, R_MLP: 2, R_GN1: 2}
-AG_CHUNKS = {N1: 4, GH: 1, N2: 1, GH1: 2, GF: 1, GAIN_M: 1, GAIN_A: 1}
+RS_CHUNKS = {R_EMB: 4, R_ATT: 4, R_GN2: 4, R_MLP: 2, R_GN1: 4}
+AG_CHUNKS = {N1: 4, GH: 1, N2: 4, GH1: 4, GF: 4}
 
 
 def dot(a, b, dims=(((1,), (0,)), ((), ()))):
@@ -39,7 +39,7 @@
                  h_tok, h_pos, h_invf, h_ga, h_gm, h_gh, emb, wq4, wk, wv, wo, wg, wu, wd,
                  o_n1, o_n2, o_gh, o_gh1, o_gf, act, gcat, heads, gqkv, gain_m, gain_a, hid,
                  tok, pos, invf, ga, gm, gh_in, embv, onehot, wqr, wqf, wqkv, wov, wguv, wdv, pb, rd, sb, rr,
-                 x0g, wgut, wqkvt, x0f, nrm1, nrm2, h1f, gh1f, inv, gact, qkvb, tabs, probs,
+                 x0g, h1g, gn2g, gn1g, wgut, wqkvt, x0f, h1f, inv, gact, qkvb, tabs, probs,
                  ag_s, ag_r, rs_s, rs_r, loc):
     chips = n_tp // 2
     seq = h_tok.shape[1]
@@ -104,8 +104,8 @@
     near = sorted(range(1, chips), key=lambda d: min(d, chips - d))
     incoming = [(d, c) for d in near for c in (1, 0)]
 
-    ag_set = {N1: 0, N2: 0, GH1: 0, GF: 0, GH: 1, GAIN_M: 1, GAIN_A: 1}
-    ag = {N1: x0g, GH: o_gh, N2: o_n2, GH1: o_gh1, GF: o_gf, GAIN_M: gain_m, GAIN_A: gain_a}
+    ag_set = {N1: 0, N2: 0, GH1: 0, GF: 0, GH: 1}
+    ag = {N1: x0g, GH: o_gh, N2: h1g, GH1: gn2g, GF: gn1g}
     per = 2 * chips - 1
 
     def ag_view(p, t, j):
@@ -245,15 +245,47 @@
         def _():
             fn()
 
-    def norm_fwd(x, gain):
-        r = lax.rsqrt(jnp.mean(x * x, axis=-1, keepdims=True) + RMS_EPS)
-        n = x * r
-        return (n * gain).astype(BF), n, r
-
-    def norm_bwd(g, n, r, gain):
-        part = jnp.sum(g * n, axis=0, keepdims=True)
-        scaled = g * gain
-        return r * (scaled - n * jnp.mean(scaled * n, axis=-1, keepdims=True)), part
+    def spread(v):
+        return jnp.broadcast_to(v, (seq, hd))
+
+    def norm_fwd(p, slot, gain, out, early=None):
+        square = None
+        for j in range(AG_CHUNKS[p]):
+            ag_finish(j, p, early=early if j == 0 else None)
+            part = gathered(p, j).astype(F32)
+            part = jnp.sum(part * part, axis=-1, keepdims=True)
+            square = part if square is None else square + part
+        r = lax.rsqrt(square * (1.0 / dim) + RMS_EPS)
+        inv[slot] = spread(r)
+        w = dim // AG_CHUNKS[p]
+        for j in range(AG_CHUNKS[p]):
+            c = slice(j * w, (j + 1) * w)
+            out[:, :, c] = (gathered(p, j).astype(F32) * r * gain[:, c]).astype(BF).reshape(n_tp, blk, w)
+
+    def norm_bwd(p, p_in, slot, gain, around, out, gain_out, early=None, use=None):
+        w = dim // AG_CHUNKS[p]
+        r = inv[slot][:, :1]
+        both = None
+        for j in range(AG_CHUNKS[p]):
+            c = slice(j * w, (j + 1) * w)
+            ag_finish(j, p, early=early if j == 0 else None)
+            if j == 0 and early is not None:
+                on_core(1, early)
+            g = gathered(p, j).astype(F32)
+            n = gathered(p_in, j).astype(F32) * r
+            gn = g * n
+            gain_out[:, c] = jnp.sum(gn, axis=0, keepdims=True)
+            part = jnp.sum(gn * gain[:, c], axis=-1, keepdims=True)
+            both = part if both is None else both + part
+        mean = both * (1.0 / dim)
+        for j in range(AG_CHUNKS[p]):
+            c = slice(j * w, (j + 1) * w)
+            n = gathered(p_in, j).astype(F32) * r
+            g_in = r * (gathered(p, j).astype(F32) * gain[:, c] - n * mean)
+            total = (around[:, :, c].reshape(seq, w).astype(F32) + g_in).astype(BF)
+            out[:, :, c] = total.reshape(n_tp, blk, w)
+            if use is not None:
+                use(total, c)
 
     w_cp = {}
 
@@ -290,10 +322,6 @@
         x0f[:, rs_cols(R_EMB, j)] = part
         x0g[me, :, rs_cols(R_EMB, j)] = part.astype(BF)
         ag_start(N1, j)
-    x0 = x0f[...]
-    n1b, n1, r1 = norm_fwd(x0, ga[...])
-    nrm1[...] = n1
-    inv[0] = jnp.broadcast_to(r1, (blk, hd))
     o_gh[me] = gh_in[...]
     w_cp['k'].wait()
     w_cp['v'].wait()
@@ -312,17 +340,7 @@
     def rotate(v, sign):
         return v * tabs[0] + sign * (pltpu.roll(v, hd // 2, 1) * tabs[1])
 
-    square = None
-    for j in range(AG_CHUNKS[N1]):
-        ag_finish(j, N1, early=(lambda: ag_start(GH)) if j == 0 else None)
-        part = gathered(N1, j).astype(F32)
-        part = jnp.sum(part * part, axis=-1, keepdims=True)
-        square = part if square is None else square + part
-    rms = lax.rsqrt(square * (1.0 / dim) + RMS_EPS)
-    cw = dim // AG_CHUNKS[N1]
-    for j in range(AG_CHUNKS[N1]):
-        c = slice(j * cw, (j + 1) * cw)
-        o_n1[:, :, c] = (gathered(N1, j).astype(F32) * rms * ga[:, c]).astype(BF).reshape(n_tp, blk, cw)
+    norm_fwd(N1, 0, ga, o_n1, early=lambda: ag_start(GH))
     qkv = dot(o_n1[...].reshape(seq, dim), wqkv[...])
     on_core(1, lambda: ag_start(GH))
     for h in range(local_heads + 1):
@@ -350,24 +368,27 @@
     ag_finish(0, GH)
     w_cp['d'].wait()
 
-    h1 = (x0f[...] + rs_finish(R_ATT).astype(BF).astype(F32)).astype(BF).astype(F32)
-    h1f[...] = h1
-    n2b, n2, r2 = norm_fwd(h1, gm[...])
-    o_n2[me] = n2b
-    nrm2[...] = n2
-    inv[1] = jnp.broadcast_to(r2, (blk, hd))
     ag_wait_sends(N1)
-    ag_start(N2)
-    with jax.named_scope('gact'):
-        gact[...] = dot(gathered(GH), wdv[...], NT).astype(BF).astype(F32)
-
-    ag_finish(0, N2)
+    aw = 256
+    for j in range(RS_CHUNKS[R_ATT]):
+        c = rs_cols(R_ATT, j)
+        h1 = (x0f[:, c] + rs_finish(R_ATT, j).astype(BF).astype(F32)).astype(BF)
+        h1f[:, c] = h1.astype(F32)
+        h1g[me, :, c] = h1
+        ag_start(N2, j)
+        if j * aw < ffn:
+            with jax.named_scope('gact'):
+                k = slice(j * aw, (j + 1) * aw)
+                gact[:, k] = dot(gathered(GH), wdv[k, :], NT).astype(BF).astype(F32)
+    norm_fwd(N2, 1, gm, o_n2)
+
+    n2 = o_n2[...].reshape(seq, dim)
     fw = 256
     for j in range(ffn // fw):
         c = slice(j * fw, (j + 1) * fw)
         cu = slice(ffn + j * fw, ffn + (j + 1) * fw)
-        gate = dot(gathered(N2), wguv[:, c])
-        up = dot(gathered(N2), wguv[:, cu])
+        gate = dot(n2, wguv[:, c])
+        up = dot(n2, wguv[:, cu])
         sig = jax.nn.sigmoid(gate)
         ga_act = gate * sig
         act[:, c] = (ga_act * up).astype(BF)
@@ -379,23 +400,18 @@
     for j in range(RS_CHUNKS[R_MLP]):
         rs_local(R_MLP, j, dot(act[...], wdv[:, rs_cols(R_MLP, j)]))
 
-    gn2 = rs_finish(R_GN2).astype(BF).astype(F32)
-    g_in, gain_part = norm_bwd(gn2, nrm2[...], inv[1][:, :1], gm[...])
-    gain_m[me] = gain_part
-    gh1 = (gh_in[...].astype(F32) + g_in).astype(BF)
-    gh1f[...] = gh1.astype(F32)
-    o_gh1[me] = gh1
     ag_wait_sends(N2)
-    ag_start(GH1)
-    ag_wait_sends(GH)
-    ag_start(GAIN_M)
+    for j in range(RS_CHUNKS[R_GN2]):
+        gn2g[me, :, rs_cols(R_GN2, j)] = rs_finish(R_GN2, j).astype(BF)
+        ag_start(GH1, j)
+
     def mlp_cross():
         for j in range(RS_CHUNKS[R_MLP]):
             rs_cross(R_MLP, j)
 
-    ghd = gathered_dot(GH1, lambda a, k: dot(a, wov[:, k], NT), mlp_cross).astype(BF)
-    on_core(1, mlp_cross)
-    ag_finish(0, GAIN_M, collect=False)
+    ghd_parts = []
+    norm_bwd(GH1, N2, 1, gm, o_gh, o_gh1, gain_m, early=mlp_cross, use=lambda a, c: ghd_parts.append(dot(a, wov[:, c], NT)))
+    ghd = sum(ghd_parts[1:], ghd_parts[0]).astype(BF)
 
     gv = jnp.zeros((seq, hd), F32)
     gk = jnp.zeros((seq, hd), F32)
@@ -410,31 +426,26 @@
         gqkv[:, h * hd:(h + 1) * hd] = rotate(gq, -1.0).astype(BF)
     gqkv[:, qw:qw + hd] = rotate(gk.astype(BF).astype(F32), -1.0).astype(BF)
     gqkv[:, qw + hd:] = gv.astype(BF)
-    ag_finish(0, GAIN_M, forward=False)
     rs_wait_sends(R_GN2)
     rs_start(R_GN1, lambda c: dot(gqkv[...], wqkvt[:, c]))
+
+    ag_wait_sends(GH1)
+    for j in range(RS_CHUNKS[R_GN1]):
+        gn1g[me, :, rs_cols(R_GN1, j)] = rs_finish(R_GN1, j).astype(BF)
+        ag_start(GF, j)
     hid[...] = (h1f[...] + rs_finish(R_MLP).astype(BF).astype(F32)).astype(BF)
-
-    gn1 = rs_finish(R_GN1).astype(BF).astype(F32)
-    g_in, gain_part = norm_bwd(gn1, nrm1[...], inv[0][:, :1], ga[...])
-    gain_a[me] = gain_part
-    o_gf[me] = (gh1f[...] + g_in).astype(BF)
-    ag_wait_sends(GAIN_M)
-    ag_wait_sends(GH1)
-    ag_start(GAIN_A)
-    ag_start(GF)
-    ag_finish(0, GAIN_A, GF)
+    norm_bwd(GF, N1, 0, ga, o_gh1, o_gf, gain_a)
     with jax.named_scope('tail_send'):
         rs_wait_sends(R_GN1)
         rs_wait_sends(R_MLP)
-        ag_wait_sends(GAIN_A)
+        ag_wait_sends(GH)
         ag_wait_sends(GF)
 
 
 def grads_kernel(n_tp, local_heads,
                  tok, gain_m, gain_a, hid, gh, act, n2, gcat, gh1, heads, n1, gqkv, gf,
                  o_hid, o_emb, o_wq, o_wk, o_wv, o_wo, o_wg, o_wu, o_wd, o_ga, o_gm,
-                 gains, wide, tall, qbuf, kvbuf, s_wide, s_tall, s_qkv, s_out):
+                 wide, tall, qbuf, kvbuf, s_wide, s_tall, s_qkv, s_out):
     seq, dim = n1.shape
     rows = o_emb.shape[0]
     ffn = act.shape[1]
@@ -485,14 +496,9 @@
                 tall[slot] = fn()
                 put(('t', slot), tall.at[slot], dst, s_tall.at[slot])
             it += 1
-    for i, part in enumerate((gain_a, gain_m)):
-        total = part[0]
-        for t in range(1, n_tp):
-            total = total + part[t]
-        gains[i:i + 1, :] = total
     put(('out', 0), hid, o_hid, s_out.at[0])
-    put(('out', 1), gains.at[pl.ds(0, 1)], o_ga, s_out.at[1])
-    put(('out', 2), gains.at[pl.ds(1, 1)], o_gm, s_out.at[2])
+    put(('out', 1), gain_a, o_ga, s_out.at[1])
+    put(('out', 2), gain_m, o_gm, s_out.at[2])
     qw = local_heads * hd
     with jax.named_scope('qkv'):
         for h in range(local_heads):
@@ -537,7 +543,7 @@
             functools.partial(layer_kernel, n_tp, lh),
             name='layer',
             out_shape=[sds((n_tp, blk, dim))] * 5 + [sds((seq, ffn)), sds((seq, 2 * ffn)), sds((seq, lh * hd)), sds((seq, qkvw)),
-                                                    sds((n_tp, 1, dim), F32), sds((n_tp, 1, dim), F32), sds((blk, dim))],
+                                                    sds((1, dim), F32), sds((1, dim), F32), sds((blk, dim))],
             in_specs=[hb] * 14,
             out_specs=[vm] * 12,
             scratch_shapes=[
@@ -547,8 +553,9 @@
                 pltpu.VMEM((dim, qkvw), BF), pltpu.VMEM((lh * hd, dim), BF), pltpu.VMEM((dim, 2 * ffn), BF), pltpu.VMEM((ffn, dim), BF),
                 pltpu.VMEM((5, chips, 2, blk, dim), BF), pltpu.VMEM((5, chips, blk, dim), BF),
                 pltpu.VMEM((5, chips, blk, dim), BF), pltpu.VMEM((5, chips - 1, blk, dim), BF),
-                pltpu.VMEM((n_tp, blk, dim), BF), pltpu.VMEM((2 * ffn, dim), BF), pltpu.VMEM((qkvw, dim), BF), pltpu.VMEM((blk, dim), F32), pltpu.VMEM((blk, dim), F32), pltpu.VMEM((blk, dim), F32), pltpu.VMEM((blk, dim), F32),
-                pltpu.VMEM((blk, dim), F32), pltpu.VMEM((2, blk, hd), F32), pltpu.VMEM((seq, ffn), F32), pltpu.VMEM((seq, qkvw), BF),
+                pltpu.VMEM((n_tp, blk, dim), BF), pltpu.VMEM((n_tp, blk, dim), BF), pltpu.VMEM((n_tp, blk, dim), BF),
+                pltpu.VMEM((n_tp, blk, dim), BF), pltpu.VMEM((2 * ffn, dim), BF), pltpu.VMEM((qkvw, dim), BF), pltpu.VMEM((blk, dim), F32), pltpu.VMEM((blk, dim), F32),
+                pltpu.VMEM((2, seq, hd), F32), pltpu.VMEM((seq, ffn), F32), pltpu.VMEM((seq, qkvw), BF),
                 pltpu.VMEM((2, seq, hd), F32), pltpu.VMEM((lh, seq, seq), F32),
                 pltpu.SemaphoreType.DMA((2, 2)), pltpu.SemaphoreType.DMA(((max(AG_CHUNKS.values()) + 1) * (2 * chips - 1),)),
                 pltpu.SemaphoreType.DMA((2, 2)), pltpu.SemaphoreType.DMA((2, maxc, chips)),
@@ -571,7 +578,6 @@
             in_specs=[vm] * 13,
             out_specs=[hb] * 11,
             scratch_shapes=[
-                pltpu.VMEM((2, dim), F32),
                 pltpu.VMEM((3, wide_rows, dim), F32), pltpu.VMEM((3, tall_rows, ffn), F32), pltpu.VMEM((dim * lh, hd), F32),
                 pltpu.VMEM((2, dim, hd), F32),
                 pltpu.SemaphoreType.DMA((3,)), pltpu.SemaphoreType.DMA((3,)), pltpu.SemaphoreType.DMA((3,)),

time: 74.3 us -> 69.1 us (0.930)
  Pallas kernels: 73.4 us -> 68.2 us
    pallas_call x1, Pallas kernels: 59.4 us -> 54.2 us  [device_fn(): pl.pallas_call(functools.partial(layer_kernel, n_tp, lh), name='layer', o...]
where the time goes in v5:
time: 69.1 us; the launch traced here: 69 us
  Pallas kernels  68.2 us (99%)
  between operations  0.83 us (1%)
    pallas_call x1, Pallas kernels, device_fn(): pl.pallas_call(functools.partial(layer_kernel, n_tp, lh), name='layer', o...  54.2 us
    pallas_call x1, Pallas kernels, device_fn(): pl.pallas_call(functools.partial(grads_kernel, n_tp, lh), name='grads', o...  14 us

profile of v5, /device:TPU:81, one launch (start us, length us, event | category | flops | bytes accessed | tf_op | source)
XLA Modules:
  0.0 69.0 jit_solution(15042919903753099598)
XLA Ops:
  0.6 0.0 copy-start
  0.7 54.2 %layer.1 = (bf16[8,16,2048]{2,1,0:T(8,128)(2,1)S(1)}, bf16[8,16,2048]{2,1,0:T(8,128)(2,1)S(1)}, bf16[8,16,2048]{2,1,0:T(8,128)(2,1)S(1)}, bf16[8,16,2048]{2,1,0:...) custom-call(s32[1,128]{1,0:T(1,128)} %tok.1, ...), custom_call_target="tpu_custom_call" | custom-call | tf_op jit(solution)/shard_map/layer/pallas_call | solution.py:542
  54.8 0.0 copy-done
  54.8 14.0 %grads.1 = (bf16[16,2048]{1,0:T(8,128)(2,1)}, f32[2048,2048]{1,0:T(8,128)}, f32[4096,128]{1,0:T(8,128)}, f32[2048,128]{1,0:T(8,128)}, f32[2048,128]{1,0:T(8,128)...) custom-call(s32[1,128]{1,0:T(1,128)S(1)} %copy-done, ...), custom_call_target="tpu_custom_call" | custom-call | tf_op jit(solution)/shard_map/grads/pallas_call | solution.py:572
Async XLA Ops:
  0.6 54.2 %copy-start = (s32[1,128]{1,0:T(1,128)S(1)}, s32[1,128]{1,0:T(1,128)}, u32[]{:S(2)}) copy-start(s32[1,128]{1,0:T(1,128)} %tok.1) | copy-start | bytes 1540

commit v6 on v5

--- a/solution.py
+++ b/solution.py
@@ -39,7 +39,7 @@
                  h_tok, h_pos, h_invf, h_ga, h_gm, h_gh, emb, wq4, wk, wv, wo, wg, wu, wd,
                  o_n1, o_n2, o_gh, o_gh1, o_gf, act, gcat, heads, gqkv, gain_m, gain_a, hid,
                  tok, pos, invf, ga, gm, gh_in, embv, onehot, wqr, wqf, wqkv, wov, wguv, wdv, pb, rd, sb, rr,
-                 x0g, h1g, gn2g, gn1g, wgut, wqkvt, x0f, h1f, inv, gact, qkvb, tabs, probs,
+                 x0g, h1g, gn2g, gn1g, wgut, wqkvt, wovt, x0f, h1f, inv, gact, qkvb, tabs, probs,
                  ag_s, ag_r, rs_s, rs_r, loc):
     chips = n_tp // 2
     seq = h_tok.shape[1]
@@ -136,7 +136,7 @@
             send(mine, mine, ag_s.at[q, 0], ag_recv(p, j, 0), sib)
 
     @scoped('ag_finish')
-    def ag_finish(j, *ps, early=None, forward=True, collect=True):
+    def ag_finish(j, *ps, early=None, forward=True, collect=True, between=None):
         if j == 0 and forward:
             @pl.when(core == 1)
             def _():
@@ -147,6 +147,10 @@
                             q = ag_set[p]
                             remote(got, got, ag_s.at[q, 1], ag_recv(p, k, 2 * d - c), sib).wait_recv()
                             send(got, got, ag_s.at[q, 1], ag_recv(p, k, 2 * d - c), sib)
+                    if early is not None and k == 1:
+                        early()
+                    if between is not None and k < AG_CHUNKS[ps[0]] - 1:
+                        between(k)
 
         if not collect:
             return
@@ -248,10 +252,12 @@
     def spread(v):
         return jnp.broadcast_to(v, (seq, hd))
 
-    def norm_fwd(p, slot, gain, out, early=None):
+    def norm_fwd(p, slot, gain, out, early=None, between=None):
         square = None
         for j in range(AG_CHUNKS[p]):
-            ag_finish(j, p, early=early if j == 0 else None)
+            ag_finish(j, p, early=early if j == 0 else None, between=between)
+            if between is not None and j < AG_CHUNKS[p] - 1:
+                on_core(0, lambda: between(j))
             part = gathered(p, j).astype(F32)
             part = jnp.sum(part * part, axis=-1, keepdims=True)
             square = part if square is None else square + part
@@ -269,8 +275,6 @@
         for j in range(AG_CHUNKS[p]):
             c = slice(j * w, (j + 1) * w)
             ag_finish(j, p, early=early if j == 0 else None)
-            if j == 0 and early is not None:
-                on_core(1, early)
             g = gathered(p, j).astype(F32)
             n = gathered(p_in, j).astype(F32) * r
             gn = g * n
@@ -340,9 +344,17 @@
     def rotate(v, sign):
         return v * tabs[0] + sign * (pltpu.roll(v, hd // 2, 1) * tabs[1])
 
-    norm_fwd(N1, 0, ga, o_n1, early=lambda: ag_start(GH))
+    w_cp['g'].wait()
+    w_cp['u'].wait()
+
+    def transpose_gate_up(k):
+        with jax.named_scope('wgut'):
+            n = 2 * ffn // tw
+            for b in range(n * k // 3, n * (k + 1) // 3):
+                wgut[b * tw:(b + 1) * tw, :] = dot(eye, wguv[:, b * tw:(b + 1) * tw], NT).astype(BF)
+
+    norm_fwd(N1, 0, ga, o_n1, early=lambda: ag_start(GH), between=transpose_gate_up)
     qkv = dot(o_n1[...].reshape(seq, dim), wqkv[...])
-    on_core(1, lambda: ag_start(GH))
     for h in range(local_heads + 1):
         qkvb[:, h * hd:(h + 1) * hd] = rotate(qkv[:, h * hd:(h + 1) * hd], 1.0).astype(BF)
     qkvb[:, qw + hd:] = qkv[:, qw + hd:].astype(BF)
@@ -360,27 +372,27 @@
     rs_wait_sends(R_EMB)
     rs_start(R_ATT, lambda c: dot(heads[...], wov[:, c]))
 
-    w_cp['g'].wait()
-    w_cp['u'].wait()
-    with jax.named_scope('wgut'):
-        for b in range(2 * ffn // tw):
-            wgut[b * tw:(b + 1) * tw, :] = dot(eye, wguv[:, b * tw:(b + 1) * tw], NT).astype(BF)
-    ag_finish(0, GH)
+    with jax.named_scope('wovt'):
+        for b in range(dim // tw):
+            wovt[b * tw:(b + 1) * tw, :] = dot(eye, wov[:, b * tw:(b + 1) * tw], NT).astype(BF)
+    ag_finish(0, GH, collect=False)
     w_cp['d'].wait()
 
     ag_wait_sends(N1)
-    aw = 256
     for j in range(RS_CHUNKS[R_ATT]):
         c = rs_cols(R_ATT, j)
         h1 = (x0f[:, c] + rs_finish(R_ATT, j).astype(BF).astype(F32)).astype(BF)
         h1f[:, c] = h1.astype(F32)
         h1g[me, :, c] = h1
         ag_start(N2, j)
-        if j * aw < ffn:
+    ag_finish(0, GH, forward=False)
+
+    def act_grad(k):
+        if k == 0:
             with jax.named_scope('gact'):
-                k = slice(j * aw, (j + 1) * aw)
-                gact[:, k] = dot(gathered(GH), wdv[k, :], NT).astype(BF).astype(F32)
-    norm_fwd(N2, 1, gm, o_n2)
+                gact[...] = dot(gathered(GH), wdv[...], NT).astype(BF).astype(F32)
+
+    norm_fwd(N2, 1, gm, o_n2, between=act_grad)
 
     n2 = o_n2[...].reshape(seq, dim)
     fw = 256
@@ -410,7 +422,7 @@
             rs_cross(R_MLP, j)
 
     ghd_parts = []
-    norm_bwd(GH1, N2, 1, gm, o_gh, o_gh1, gain_m, early=mlp_cross, use=lambda a, c: ghd_parts.append(dot(a, wov[:, c], NT)))
+    norm_bwd(GH1, N2, 1, gm, o_gh, o_gh1, gain_m, early=mlp_cross, use=lambda a, c: ghd_parts.append(dot(a, wovt[c, :])))
     ghd = sum(ghd_parts[1:], ghd_parts[0]).astype(BF)
 
     gv = jnp.zeros((seq, hd), F32)
@@ -554,7 +566,7 @@
                 pltpu.VMEM((5, chips, 2, blk, dim), BF), pltpu.VMEM((5, chips, blk, dim), BF),
                 pltpu.VMEM((5, chips, blk, dim), BF), pltpu.VMEM((5, chips - 1, blk, dim), BF),
                 pltpu.VMEM((n_tp, blk, dim), BF), pltpu.VMEM((n_tp, blk, dim), BF), pltpu.VMEM((n_tp, blk, dim), BF),
-                pltpu.VMEM((n_tp, blk, dim), BF), pltpu.VMEM((2 * ffn, dim), BF), pltpu.VMEM((qkvw, dim), BF), pltpu.VMEM((blk, dim), F32), pltpu.VMEM((blk, dim), F32),
+                pltpu.VMEM((n_tp, blk, dim), BF), pltpu.VMEM((2 * ffn, dim), BF), pltpu.VMEM((qkvw, dim), BF), pltpu.VMEM((dim, lh * hd), BF), pltpu.VMEM((blk, dim), F32), pltpu.VMEM((blk, dim), F32),
                 pltpu.VMEM((2, seq, hd), F32), pltpu.VMEM((seq, ffn), F32), pltpu.VMEM((seq, qkvw), BF),
                 pltpu.VMEM((2, seq, hd), F32), pltpu.VMEM((lh, seq, seq), F32),
                 pltpu.SemaphoreType.DMA((2, 2)), pltpu.SemaphoreType.DMA(((max(AG_CHUNKS.values()) + 1) * (2 * chips - 1),)),

time: 69.1 us -> 67.6 us (0.978)
  Pallas kernels: 68.2 us -> 66.7 us
    pallas_call x1, Pallas kernels: 54.2 us -> 52.7 us  [device_fn(): pl.pallas_call(functools.partial(layer_kernel, n_tp, lh), name='layer', o...]
where the time goes in v6:
time: 67.6 us
  Pallas kernels  66.7 us (99%)
  between operations  0.85 us (1%)
    pallas_call x1, Pallas kernels, device_fn(): pl.pallas_call(functools.partial(layer_kernel, n_tp, lh), name='layer', o...  52.7 us
    pallas_call x1, Pallas kernels, device_fn(): pl.pallas_call(functools.partial(grads_kernel, n_tp, lh), name='grads', o...  14 us

profile of v6, /device:TPU:81, one launch (start us, length us, event | category | flops | bytes accessed | tf_op | source)
XLA Modules:
  0.0 67.6 jit_solution(1564960036317352955)
XLA Ops:
  0.6 0.0 copy-start
  0.7 52.7 %layer.1 = (bf16[8,16,2048]{2,1,0:T(8,128)(2,1)S(1)}, bf16[8,16,2048]{2,1,0:T(8,128)(2,1)S(1)}, bf16[8,16,2048]{2,1,0:T(8,128)(2,1)S(1)}, bf16[8,16,2048]{2,1,0:...) custom-call(s32[1,128]{1,0:T(1,128)} %tok.1, ...), custom_call_target="tpu_custom_call" | custom-call | tf_op jit(solution)/shard_map/layer/pallas_call | solution.py:554
  53.3 0.0 copy-done
  53.4 14.0 %grads.1 = (bf16[16,2048]{1,0:T(8,128)(2,1)}, f32[2048,2048]{1,0:T(8,128)}, f32[4096,128]{1,0:T(8,128)}, f32[2048,128]{1,0:T(8,128)}, f32[2048,128]{1,0:T(8,128)...) custom-call(s32[1,128]{1,0:T(1,128)S(1)} %copy-done, ...), custom_call_target="tpu_custom_call" | custom-call | tf_op jit(solution)/shard_map/grads/pallas_call | solution.py:584
Async XLA Ops:
  0.6 52.7 %copy-start = (s32[1,128]{1,0:T(1,128)S(1)}, s32[1,128]{1,0:T(1,128)}, u32[]{:S(2)}) copy-start(s32[1,128]{1,0:T(1,128)} %tok.1) | copy-start | bytes 1540

commit v7 on v6

--- a/solution.py
+++ b/solution.py
@@ -101,8 +101,7 @@
     def send(*args):
         remote(*args).start()
 
-    near = sorted(range(1, chips), key=lambda d: min(d, chips - d))
-    incoming = [(d, c) for d in near for c in (1, 0)]
+    incoming = [(d, c) for d in order for c in (1, 0)]
 
     ag_set = {N1: 0, N2: 0, GH1: 0, GF: 0, GH: 1}
     ag = {N1: x0g, GH: o_gh, N2: h1g, GH1: gn2g, GF: gn1g}
@@ -457,7 +456,7 @@
 def grads_kernel(n_tp, local_heads,
                  tok, gain_m, gain_a, hid, gh, act, n2, gcat, gh1, heads, n1, gqkv, gf,
                  o_hid, o_emb, o_wq, o_wk, o_wv, o_wo, o_wg, o_wu, o_wd, o_ga, o_gm,
-                 wide, tall, qbuf, kvbuf, s_wide, s_tall, s_qkv, s_out):
+                 wide, tall, qbuf, kvbuf, s_wide, s_tall, s_qkv, s_out, s_first):
     seq, dim = n1.shape
     rows = o_emb.shape[0]
     ffn = act.shape[1]
@@ -496,9 +495,19 @@
             slot = iw % n_wide
             fn, dst = wide_units[iw]
             free(('w', slot))
+            if iw == n_wide:
+                for k in range(4):
+                    free(('f', k))
             with jax.named_scope(f'wide_{iw}'):
-                wide[slot] = fn()
-                put(('w', slot), wide.at[slot], dst, s_wide.at[slot])
+                if iw == 0:
+                    fr = wr // 4
+                    for k in range(4):
+                        rows_k = slice(k * fr, (k + 1) * fr)
+                        wide[slot, rows_k] = dot(act[:, rows_k], gh[...], TN)
+                        put(('f', k), wide.at[slot, pl.ds(k * fr, fr)], o_wd.at[pl.ds(k * fr, fr)], s_first.at[k])
+                else:
+                    wide[slot] = fn()
+                    put(('w', slot), wide.at[slot], dst, s_wide.at[slot])
             iw += 1
         if it < len(tall_units):
             slot = it % n_tall
@@ -593,7 +602,7 @@
                 pltpu.VMEM((3, wide_rows, dim), F32), pltpu.VMEM((3, tall_rows, ffn), F32), pltpu.VMEM((dim * lh, hd), F32),
                 pltpu.VMEM((2, dim, hd), F32),
                 pltpu.SemaphoreType.DMA((3,)), pltpu.SemaphoreType.DMA((3,)), pltpu.SemaphoreType.DMA((3,)),
-                pltpu.SemaphoreType.DMA((3,)),
+                pltpu.SemaphoreType.DMA((3,)), pltpu.SemaphoreType.DMA((4,)),
             ],
             compiler_params=pltpu.CompilerParams(vmem_limit_bytes=24 * 1024 * 1024),
         )(tokens, gain_m, gain_a, hid, gh, act, n2, gcat, gh1, heads, n1, gqkv, gf)

time: 67.6 us -> 67.4 us (level)
  no operation moved by 1% of the time
where the time goes in v7:
time: 67.4 us; the launch traced here: 67.3 us
  Pallas kernels  66.4 us (99%)
  between operations  0.85 us (1%)
    pallas_call x1, Pallas kernels, device_fn(): pl.pallas_call(functools.partial(layer_kernel, n_tp, lh), name='layer', o...  52.6 us
    pallas_call x1, Pallas kernels, device_fn(): pl.pallas_call(functools.partial(grads_kernel, n_tp, lh), name='grads', o...  13.9 us

profile of v7, /device:TPU:81, one launch (start us, length us, event | category | flops | bytes accessed | tf_op | source)
XLA Modules:
  0.0 67.3 jit_solution(4467758870773783385)
XLA Ops:
  0.6 0.0 copy-start
  0.7 52.6 %layer.1 = (bf16[8,16,2048]{2,1,0:T(8,128)(2,1)S(1)}, bf16[8,16,2048]{2,1,0:T(8,128)(2,1)S(1)}, bf16[8,16,2048]{2,1,0:T(8,128)(2,1)S(1)}, bf16[8,16,2048]{2,1,0:...) custom-call(s32[1,128]{1,0:T(1,128)} %tok.1, ...), custom_call_target="tpu_custom_call" | custom-call | tf_op jit(solution)/shard_map/layer/pallas_call | solution.py:563
  53.2 0.0 copy-done
  53.3 13.9 %grads.1 = (bf16[16,2048]{1,0:T(8,128)(2,1)}, f32[2048,2048]{1,0:T(8,128)}, f32[4096,128]{1,0:T(8,128)}, f32[2048,128]{1,0:T(8,128)}, f32[2048,128]{1,0:T(8,128)...) custom-call(s32[1,128]{1,0:T(1,128)S(1)} %copy-done, ...), custom_call_target="tpu_custom_call" | custom-call | tf_op jit(solution)/shard_map/grads/pallas_call | solution.py:593
Async XLA Ops:
  0.6 52.6 %copy-start = (s32[1,128]{1,0:T(1,128)S(1)}, s32[1,128]{1,0:T(1,128)}, u32[]{:S(2)}) copy-start(s32[1,128]{1,0:T(1,128)} %tok.1) | copy-start | bytes 1540
